TPU v7x, 32 devices: a 4x4x1 block of a 4x4x8 slice. The times are simulated.
32 devices in a mesh: videos: 1 (over z), tokens: 4 (over y), frames: 8 (over x, core).
Axes of the slice: x: 4, y: 4, z: 1, core: 2. Of those that a mesh axis runs over, the one named last changes fastest.
The devices are a block of a 4x4x8 slice.
Arguments:
- z_queue: float32 [128, 256, 4], P(('videos', 'frames'), 'tokens')
- ada_mod: float32 [128, 2, 6, 768], P(('videos', 'frames'))
- step_size: float32 [128], P(('videos', 'frames'))
- new_noise: float32 [6, 256, 4], P('videos', 'tokens')
- lag_bias: float32 [2, 12, 16], replicated
- w_in: bfloat16 [4, 768], replicated
- w_out: bfloat16 [768, 4], replicated
- w_sqkv: bfloat16 [2, 768, 3, 12, 64], replicated
- w_so: bfloat16 [2, 12, 64, 768], replicated
- w_tqkv: bfloat16 [2, 768, 3, 12, 64], replicated
- w_to: bfloat16 [2, 12, 64, 768], replicated
- w_up: bfloat16 [2, 768, 3072], replicated
- w_down: bfloat16 [2, 3072, 768], replicated
Outputs:
- output 1: float32 [6, 256, 4], P('videos', ('tokens', 'frames'))
- output 2: float32 [128, 256, 4], P(('videos', 'frames'), 'tokens')
All inputs are finite; a program needn't handle non-finite values.
Results may differ from a plain program's by a relative error of at most 0.0155034.
Values are sent between devices in bfloat16 or wider.
A program may use at most 768 MiB of HBM per device.

v0:
```python
import jax
import jax.numpy as jnp
from jax import lax
from jax.sharding import PartitionSpec as P


def layer_norm(xres):
    row_mean = jnp.mean(xres, axis=-1, keepdims=True)
    centered = xres - row_mean
    row_var = jnp.mean(centered * centered, axis=-1, keepdims=True)
    return centered * lax.rsqrt(row_var + 1e-6)


def modulate(xres, mod_l, which):
    shift_vec = mod_l[..., None, 2 * which, :]
    scale_vec = mod_l[..., None, 2 * which + 1, :]
    return (layer_norm(xres) * (1.0 + scale_vec) + shift_vec).astype(jnp.bfloat16)


def spatial_block(u_act, w_qkv, w_proj):
    qkv_loc = jnp.einsum('apd,dthe->apthe', u_act, w_qkv, preferred_element_type=jnp.float32).astype(jnp.bfloat16)
    qkv_full = lax.all_to_all(qkv_loc, 'tokens', 3, 1, tiled=True)
    head_dim = qkv_full.shape[-1]
    scores = jnp.einsum('aqhe,akhe->ahqk', qkv_full[:, :, 0], qkv_full[:, :, 1], preferred_element_type=jnp.float32) * head_dim ** -0.5
    attn_prob = jax.nn.softmax(scores, axis=-1).astype(jnp.bfloat16)
    attn_out = jnp.einsum('ahqk,akhe->aqhe', attn_prob, qkv_full[:, :, 2], preferred_element_type=jnp.float32).astype(jnp.bfloat16)
    attn_loc = lax.all_to_all(attn_out, 'tokens', 1, 2, tiled=True)
    return jnp.einsum('aphe,hed->apd', attn_loc, w_proj, preferred_element_type=jnp.float32)


def temporal_qkv(u_act, w_qkv):
    return jnp.einsum('apd,dthe->apthe', u_act, w_qkv, preferred_element_type=jnp.float32).astype(jnp.bfloat16)


def temporal_attend(qkv_loc, halo_kv, lag_bias, w_proj, has_prev):
    n_frames = qkv_loc.shape[0]
    window = lag_bias.shape[-1]
    head_dim = qkv_loc.shape[-1]
    keys_ext = jnp.concatenate([halo_kv[:, :, 0], qkv_loc[:, :, 1]], axis=0)
    vals_ext = jnp.concatenate([halo_kv[:, :, 1], qkv_loc[:, :, 2]], axis=0)
    scores = jnp.einsum('aphe,bphe->phab', qkv_loc[:, :, 0], keys_ext, preferred_element_type=jnp.float32) * head_dim ** -0.5
    query_idx = jnp.arange(n_frames)[:, None]
    key_idx = jnp.arange(n_frames + window - 1)[None, :]
    lag_mat = query_idx + window - 1 - key_idx
    valid = (lag_mat >= 0) & (lag_mat < window) & ((key_idx >= window - 1) | has_prev)
    bias_mat = jnp.take(lag_bias, jnp.clip(lag_mat, 0, window - 1), axis=1)
    scores = jnp.where(valid, scores + bias_mat, -1e30)
    attn_prob = jax.nn.softmax(scores, axis=-1).astype(jnp.bfloat16)
    attn_out = jnp.einsum('phab,bphe->aphe', attn_prob, vals_ext, preferred_element_type=jnp.float32).astype(jnp.bfloat16)
    return jnp.einsum('aphe,hed->apd', attn_out, w_proj, preferred_element_type=jnp.float32)


def mlp_block(u_act, w_up, w_down):
    hidden = jnp.einsum('apd,dk->apk', u_act, w_up, preferred_element_type=jnp.float32)
    return jnp.einsum('apk,kd->apd', jax.nn.gelu(hidden, approximate=True).astype(jnp.bfloat16), w_down, preferred_element_type=jnp.float32)


def solution(mesh):
    n_blocks = mesh.shape['frames']
    to_next = [(i, i + 1) for i in range(n_blocks - 1)]
    to_prev = [(i + 1, i) for i in range(n_blocks - 1)]
    slot_spec = P(('videos', 'frames'), 'tokens', None)
    mod_spec = P(('videos', 'frames'), None, None, None)
    step_spec = P(('videos', 'frames'))
    noise_spec = P('videos', 'tokens', None)
    emit_spec = P('videos', ('tokens', 'frames'), None)

    def body(z_loc, mod_loc, step_loc, noise_loc, lag_bias, w_in, w_out, w_sqkv, w_so, w_tqkv, w_to, w_up, w_down):
        frame_pos = lax.axis_index('frames')
        has_prev = frame_pos > 0
        n_layers = w_sqkv.shape[0]
        window = lag_bias.shape[-1]
        n_frames = z_loc.shape[0]
        step_col = step_loc[:, None, None]

        def one_step(z_cur, noise_frame):
            xres = jnp.einsum('apc,cd->apd', z_cur.astype(jnp.bfloat16), w_in, preferred_element_type=jnp.float32).astype(jnp.bfloat16).astype(jnp.float32)
            for layer in range(n_layers):
                mod_l = mod_loc[:, layer]
                xres = xres + spatial_block(modulate(xres, mod_l, 0), w_sqkv[layer], w_so[layer])
                qkv_loc = temporal_qkv(modulate(xres, mod_l, 1), w_tqkv[layer])
                halo_kv = lax.ppermute(qkv_loc[n_frames - window + 1:, :, 1:], 'frames', to_next)
                xres = xres + temporal_attend(qkv_loc, halo_kv, lag_bias[layer], w_to[layer], has_prev)
                xres = xres + mlp_block(modulate(xres, mod_l, 2), w_up[layer], w_down[layer])
            velocity = jnp.einsum('apd,dc->apc', layer_norm(xres).astype(jnp.bfloat16), w_out, preferred_element_type=jnp.float32)
            z_new = z_cur + step_col * velocity
            incoming = lax.ppermute(z_new[0], 'frames', to_prev)
            incoming = jnp.where(frame_pos == n_blocks - 1, noise_frame, incoming)
            emit_loc = lax.psum_scatter(jnp.where(frame_pos == 0, z_new[0], 0.0), 'frames', scatter_dimension=0, tiled=True)
            return jnp.concatenate([z_new[1:], incoming[None]], axis=0), emit_loc

        z_out, emitted = lax.scan(one_step, z_loc, noise_loc)
        return emitted, z_out

    return jax.shard_map(body, mesh=mesh, in_specs=(slot_spec, mod_spec, step_spec, noise_spec) + (P(),) * 9, out_specs=(emit_spec, slot_spec), check_vma=False)
```

profile of v0, /device:TPU:97, one launch (start us, length us, event | category | flops | bytes accessed | tf_op | source)
XLA Modules:
  0.0 4594.5 jit_solution(1001367843666529763)
XLA Ops:
  4.2 4589.1 %while.16 = (s32[]{:T(128)}, f32[16,64,4]{1,2,0:T(4,128)S(1)}, f32[6,8,4]{1,2,0:T(4,128)}, f32[16,1,1]{0,2,1:T(1,128)}, bf16[4,768]{1,0:T(4,128)(2,1)}, /*index=...) while((s32[]{:T(128)}, f32[16,64,4]{1,2,0:T(4,128)S(1)}, ...), condition=%wide.region_24.26_spmd, body=%wide.region_0.25_spmd.sunk | while | flops 40650346496 | bytes 812076480 | solution.py:92
  40.4 62.5 %all_to_all.164 = bf16[4,2,294912]{2,1,0:T(2,128)(2,1)} all-to-all(bf16[4,2,294912]{2,1,0:T(2,128)(2,1)} %reshape.211), channel_id=1, replica_groups=mesh['videos'=1,'tokens'=4,'frames'=8] {'tokens'}, dimensions={0} | all-to-all | bytes 9437184 | tf_op jit(solution)/shard_map/while/body/eval_jaxpr/all_to_all | solution.py:22
  181.4 24.5 all_to_all.165
  246.8 54.4 %collective-permute-done = bf16[15,64,2,12,64]{4,1,3,0,2:T(8,128)(2,1)} collective-permute-done((bf16[15,64,2,12,64]{4,1,3,0,2:T(8,128)(2,1)}, bf16[15,64,2,12,64]{4,1,3,0,2:T(8,128)(2,1)}, u32[]{:S(2)}, u32[]{:S(2)}) %collective-permute-start) | collective-permute-done | bytes 2949152 | tf_op jit(solution)/shard_map/while/body/eval_jaxpr/ppermute | solution.py:82
  314.3 21.8 fusion.280
  416.6 35.3 all_to_all.166
  574.5 36.1 collective-permute-start.1
  617.3 56.9 %collective-permute-done.1 = bf16[15,64,2,12,64]{4,1,3,0,2:T(8,128)(2,1)} collective-permute-done((bf16[15,64,2,12,64]{4,1,3,0,2:T(8,128)(2,1)}, bf16[15,64,2,12,64]{4,1,3,0,2:T(8,128)(2,1)}, u32[]{:S(2)}, u32[]{:S(2)}) %collective-permute-start.1) | collective-permute-done | bytes 2949152 | tf_op jit(solution)/shard_map/while/body/eval_jaxpr/ppermute | solution.py:82
  687.4 21.8 fusion.289
  809.9 58.0 %all_to_all.164 = bf16[4,2,294912]{2,1,0:T(2,128)(2,1)} all-to-all(bf16[4,2,294912]{2,1,0:T(2,128)(2,1)} %reshape.211), channel_id=1, replica_groups=mesh['videos'=1,'tokens'=4,'frames'=8] {'tokens'}, dimensions={0} | all-to-all | bytes 9437184 | tf_op jit(solution)/shard_map/while/body/eval_jaxpr/all_to_all | solution.py:22
  946.4 22.2 all_to_all.165
  1012.2 54.4 %collective-permute-done = bf16[15,64,2,12,64]{4,1,3,0,2:T(8,128)(2,1)} collective-permute-done((bf16[15,64,2,12,64]{4,1,3,0,2:T(8,128)(2,1)}, bf16[15,64,2,12,64]{4,1,3,0,2:T(8,128)(2,1)}, u32[]{:S(2)}, u32[]{:S(2)}) %collective-permute-start) | collective-permute-done | bytes 2949152 | tf_op jit(solution)/shard_map/while/body/eval_jaxpr/ppermute | solution.py:82
  1079.7 21.8 fusion.280
  1182.0 35.3 all_to_all.166
  1339.9 33.3 collective-permute-start.1
  1379.9 56.9 %collective-permute-done.1 = bf16[15,64,2,12,64]{4,1,3,0,2:T(8,128)(2,1)} collective-permute-done((bf16[15,64,2,12,64]{4,1,3,0,2:T(8,128)(2,1)}, bf16[15,64,2,12,64]{4,1,3,0,2:T(8,128)(2,1)}, u32[]{:S(2)}, u32[]{:S(2)}) %collective-permute-start.1) | collective-permute-done | bytes 2949152 | tf_op jit(solution)/shard_map/while/body/eval_jaxpr/ppermute | solution.py:82
  1450.0 21.8 fusion.289
  1572.7 56.6 %all_to_all.164 = bf16[4,2,294912]{2,1,0:T(2,128)(2,1)} all-to-all(bf16[4,2,294912]{2,1,0:T(2,128)(2,1)} %reshape.211), channel_id=1, replica_groups=mesh['videos'=1,'tokens'=4,'frames'=8] {'tokens'}, dimensions={0} | all-to-all | bytes 9437184 | tf_op jit(solution)/shard_map/while/body/eval_jaxpr/all_to_all | solution.py:22
  1775.9 54.4 %collective-permute-done = bf16[15,64,2,12,64]{4,1,3,0,2:T(8,128)(2,1)} collective-permute-done((bf16[15,64,2,12,64]{4,1,3,0,2:T(8,128)(2,1)}, bf16[15,64,2,12,64]{4,1,3,0,2:T(8,128)(2,1)}, u32[]{:S(2)}, u32[]{:S(2)}) %collective-permute-start) | collective-permute-done | bytes 2949152 | tf_op jit(solution)/shard_map/while/body/eval_jaxpr/ppermute | solution.py:82
  1843.4 21.8 fusion.280
  1945.8 35.3 all_to_all.166
  2103.6 35.4 collective-permute-start.1
  2145.8 56.9 %collective-permute-done.1 = bf16[15,64,2,12,64]{4,1,3,0,2:T(8,128)(2,1)} collective-permute-done((bf16[15,64,2,12,64]{4,1,3,0,2:T(8,128)(2,1)}, bf16[15,64,2,12,64]{4,1,3,0,2:T(8,128)(2,1)}, u32[]{:S(2)}, u32[]{:S(2)}) %collective-permute-start.1) | collective-permute-done | bytes 2949152 | tf_op jit(solution)/shard_map/while/body/eval_jaxpr/ppermute | solution.py:82
  2215.9 21.8 fusion.289
  2338.3 58.8 %all_to_all.164 = bf16[4,2,294912]{2,1,0:T(2,128)(2,1)} all-to-all(bf16[4,2,294912]{2,1,0:T(2,128)(2,1)} %reshape.211), channel_id=1, replica_groups=mesh['videos'=1,'tokens'=4,'frames'=8] {'tokens'}, dimensions={0} | all-to-all | bytes 9437184 | tf_op jit(solution)/shard_map/while/body/eval_jaxpr/all_to_all | solution.py:22
  2475.6 22.8 all_to_all.165
  2540.6 54.4 %collective-permute-done = bf16[15,64,2,12,64]{4,1,3,0,2:T(8,128)(2,1)} collective-permute-done((bf16[15,64,2,12,64]{4,1,3,0,2:T(8,128)(2,1)}, bf16[15,64,2,12,64]{4,1,3,0,2:T(8,128)(2,1)}, u32[]{:S(2)}, u32[]{:S(2)}) %collective-permute-start) | collective-permute-done | bytes 2949152 | tf_op jit(solution)/shard_map/while/body/eval_jaxpr/ppermute | solution.py:82
  2608.1 21.8 fusion.280
  2710.5 35.3 all_to_all.166
  2868.3 31.2 collective-permute-start.1
  2906.3 56.9 %collective-permute-done.1 = bf16[15,64,2,12,64]{4,1,3,0,2:T(8,128)(2,1)} collective-permute-done((bf16[15,64,2,12,64]{4,1,3,0,2:T(8,128)(2,1)}, bf16[15,64,2,12,64]{4,1,3,0,2:T(8,128)(2,1)}, u32[]{:S(2)}, u32[]{:S(2)}) %collective-permute-start.1) | collective-permute-done | bytes 2949152 | tf_op jit(solution)/shard_map/while/body/eval_jaxpr/ppermute | solution.py:82
  2976.4 21.8 fusion.289
  3100.9 56.7 %all_to_all.164 = bf16[4,2,294912]{2,1,0:T(2,128)(2,1)} all-to-all(bf16[4,2,294912]{2,1,0:T(2,128)(2,1)} %reshape.211), channel_id=1, replica_groups=mesh['videos'=1,'tokens'=4,'frames'=8] {'tokens'}, dimensions={0} | all-to-all | bytes 9437184 | tf_op jit(solution)/shard_map/while/body/eval_jaxpr/all_to_all | solution.py:22
  3236.1 20.8 all_to_all.165
  3304.7 54.4 %collective-permute-done = bf16[15,64,2,12,64]{4,1,3,0,2:T(8,128)(2,1)} collective-permute-done((bf16[15,64,2,12,64]{4,1,3,0,2:T(8,128)(2,1)}, bf16[15,64,2,12,64]{4,1,3,0,2:T(8,128)(2,1)}, u32[]{:S(2)}, u32[]{:S(2)}) %collective-permute-start) | collective-permute-done | bytes 2949152 | tf_op jit(solution)/shard_map/while/body/eval_jaxpr/ppermute | solution.py:82
  3372.2 21.8 fusion.280
  3474.5 35.3 all_to_all.166
  3632.4 34.1 collective-permute-start.1
  3673.3 56.9 %collective-permute-done.1 = bf16[15,64,2,12,64]{4,1,3,0,2:T(8,128)(2,1)} collective-permute-done((bf16[15,64,2,12,64]{4,1,3,0,2:T(8,128)(2,1)}, bf16[15,64,2,12,64]{4,1,3,0,2:T(8,128)(2,1)}, u32[]{:S(2)}, u32[]{:S(2)}) %collective-permute-start.1) | collective-permute-done | bytes 2949152 | tf_op jit(solution)/shard_map/while/body/eval_jaxpr/ppermute | solution.py:82
  3743.4 21.8 fusion.289
  3865.8 58.1 %all_to_all.164 = bf16[4,2,294912]{2,1,0:T(2,128)(2,1)} all-to-all(bf16[4,2,294912]{2,1,0:T(2,128)(2,1)} %reshape.211), channel_id=1, replica_groups=mesh['videos'=1,'tokens'=4,'frames'=8] {'tokens'}, dimensions={0} | all-to-all | bytes 9437184 | tf_op jit(solution)/shard_map/while/body/eval_jaxpr/all_to_all | solution.py:22
  4002.4 22.3 all_to_all.165
  4068.1 54.4 %collective-permute-done = bf16[15,64,2,12,64]{4,1,3,0,2:T(8,128)(2,1)} collective-permute-done((bf16[15,64,2,12,64]{4,1,3,0,2:T(8,128)(2,1)}, bf16[15,64,2,12,64]{4,1,3,0,2:T(8,128)(2,1)}, u32[]{:S(2)}, u32[]{:S(2)}) %collective-permute-start) | collective-permute-done | bytes 2949152 | tf_op jit(solution)/shard_map/while/body/eval_jaxpr/ppermute | solution.py:82
  4135.6 21.8 fusion.280
  4238.0 35.3 all_to_all.166
  4395.9 32.8 collective-permute-start.1
  4435.3 56.9 %collective-permute-done.1 = bf16[15,64,2,12,64]{4,1,3,0,2:T(8,128)(2,1)} collective-permute-done((bf16[15,64,2,12,64]{4,1,3,0,2:T(8,128)(2,1)}, bf16[15,64,2,12,64]{4,1,3,0,2:T(8,128)(2,1)}, u32[]{:S(2)}, u32[]{:S(2)}) %collective-permute-start.1) | collective-permute-done | bytes 2949152 | tf_op jit(solution)/shard_map/while/body/eval_jaxpr/ppermute | solution.py:82
  4505.4 21.8 fusion.289
  (1105 shorter events, 2774.1 us)
Async XLA Ops:
  4.4 233.3 %copy-start.21 = (f32[2,12,16]{1,2,0:T(8,128)}, f32[2,12,16]{1,2,0:T(8,128)S(1)}, u32[]{:S(2)}) copy-start(f32[2,12,16]{1,2,0:T(8,128)S(1)} %get-tuple-element.784) | copy-start | bytes 4612 | tf_op jit(solution)/shard_map/while
  232.4 68.8 %collective-permute-start = (bf16[15,64,2,12,64]{4,1,3,0,2:T(8,128)(2,1)}, bf16[15,64,2,12,64]{4,1,3,0,2:T(8,128)(2,1)}, u32[]{:S(2)}, u32[]{:S(2)}) collective-permute-start(bf16[15,64,2,12,64]{4,1,3,0,2:T(8,128)(2,1)} %copy.173), channel_id=1, source_target_pairs={{0,1},{1,2},{2,3},{3,4},{4,5},{5,6},{6,7},{8,9},{9,10},{10,11},{11... | collective-permute-start | bytes 8847368 | tf_op jit(solution)/shard_map/while/body/eval_jaxpr/ppermute | solution.py:82
  240.7 95.4 %copy-start.24 = (pred[16,31]{1,0:T(8,128)(4,1)}, pred[16,31]{1,0:T(8,128)(4,1)S(1)}, u32[]{:S(2)}) copy-start(pred[16,31]{1,0:T(8,128)(4,1)S(1)} %get-tuple-element.697) | copy-start | bytes 1492 | tf_op jit(solution)/shard_map/while
  314.3 31.4 slice-start.2
  570.6 40.0 copy-start.31
  574.5 99.8 %collective-permute-start.1 = (bf16[15,64,2,12,64]{4,1,3,0,2:T(8,128)(2,1)}, bf16[15,64,2,12,64]{4,1,3,0,2:T(8,128)(2,1)}, u32[]{:S(2)}, u32[]{:S(2)}) collective-permute-start(bf16[15,64,2,12,64]{4,1,3,0,2:T(8,128)(2,1)} %copy.180), channel_id=1, source_target_pairs={{0,1},{1,2},{2,3},{3,4},{4,5},{5,6},{6,7},{8,9},{9,10},{10,11},{11... | collective-permute-start | bytes 8847368 | tf_op jit(solution)/shard_map/while/body/eval_jaxpr/ppermute | solution.py:82
  687.4 31.6 slice-start
  759.0 13.9 collective-permute-start.2
  773.8 229.3 %copy-start.21 = (f32[2,12,16]{1,2,0:T(8,128)}, f32[2,12,16]{1,2,0:T(8,128)S(1)}, u32[]{:S(2)}) copy-start(f32[2,12,16]{1,2,0:T(8,128)S(1)} %get-tuple-element.784) | copy-start | bytes 4612 | tf_op jit(solution)/shard_map/while
  995.0 71.5 %collective-permute-start = (bf16[15,64,2,12,64]{4,1,3,0,2:T(8,128)(2,1)}, bf16[15,64,2,12,64]{4,1,3,0,2:T(8,128)(2,1)}, u32[]{:S(2)}, u32[]{:S(2)}) collective-permute-start(bf16[15,64,2,12,64]{4,1,3,0,2:T(8,128)(2,1)} %copy.173), channel_id=1, source_target_pairs={{0,1},{1,2},{2,3},{3,4},{4,5},{5,6},{6,7},{8,9},{9,10},{10,11},{11... | collective-permute-start | bytes 8847368 | tf_op jit(solution)/shard_map/while/body/eval_jaxpr/ppermute | solution.py:82
  1006.1 95.4 %copy-start.24 = (pred[16,31]{1,0:T(8,128)(4,1)}, pred[16,31]{1,0:T(8,128)(4,1)S(1)}, u32[]{:S(2)}) copy-start(pred[16,31]{1,0:T(8,128)(4,1)S(1)} %get-tuple-element.697) | copy-start | bytes 1492 | tf_op jit(solution)/shard_map/while
  1079.7 31.4 slice-start.2
  1336.0 37.2 copy-start.31
  1339.9 97.0 %collective-permute-start.1 = (bf16[15,64,2,12,64]{4,1,3,0,2:T(8,128)(2,1)}, bf16[15,64,2,12,64]{4,1,3,0,2:T(8,128)(2,1)}, u32[]{:S(2)}, u32[]{:S(2)}) collective-permute-start(bf16[15,64,2,12,64]{4,1,3,0,2:T(8,128)(2,1)} %copy.180), channel_id=1, source_target_pairs={{0,1},{1,2},{2,3},{3,4},{4,5},{5,6},{6,7},{8,9},{9,10},{10,11},{11... | collective-permute-start | bytes 8847368 | tf_op jit(solution)/shard_map/while/body/eval_jaxpr/ppermute | solution.py:82
  1450.0 31.6 slice-start
  1521.6 14.1 collective-permute-start.2
  1536.6 230.2 %copy-start.21 = (f32[2,12,16]{1,2,0:T(8,128)}, f32[2,12,16]{1,2,0:T(8,128)S(1)}, u32[]{:S(2)}) copy-start(f32[2,12,16]{1,2,0:T(8,128)S(1)} %get-tuple-element.784) | copy-start | bytes 4612 | tf_op jit(solution)/shard_map/while
  1755.0 75.3 %collective-permute-start = (bf16[15,64,2,12,64]{4,1,3,0,2:T(8,128)(2,1)}, bf16[15,64,2,12,64]{4,1,3,0,2:T(8,128)(2,1)}, u32[]{:S(2)}, u32[]{:S(2)}) collective-permute-start(bf16[15,64,2,12,64]{4,1,3,0,2:T(8,128)(2,1)} %copy.173), channel_id=1, source_target_pairs={{0,1},{1,2},{2,3},{3,4},{4,5},{5,6},{6,7},{8,9},{9,10},{10,11},{11... | collective-permute-start | bytes 8847368 | tf_op jit(solution)/shard_map/while/body/eval_jaxpr/ppermute | solution.py:82
  1769.8 95.4 %copy-start.24 = (pred[16,31]{1,0:T(8,128)(4,1)}, pred[16,31]{1,0:T(8,128)(4,1)S(1)}, u32[]{:S(2)}) copy-start(pred[16,31]{1,0:T(8,128)(4,1)S(1)} %get-tuple-element.697) | copy-start | bytes 1492 | tf_op jit(solution)/shard_map/while
  1843.4 31.4 slice-start.2
  2099.8 39.3 copy-start.31
  2103.6 99.1 %collective-permute-start.1 = (bf16[15,64,2,12,64]{4,1,3,0,2:T(8,128)(2,1)}, bf16[15,64,2,12,64]{4,1,3,0,2:T(8,128)(2,1)}, u32[]{:S(2)}, u32[]{:S(2)}) collective-permute-start(bf16[15,64,2,12,64]{4,1,3,0,2:T(8,128)(2,1)} %copy.180), channel_id=1, source_target_pairs={{0,1},{1,2},{2,3},{3,4},{4,5},{5,6},{6,7},{8,9},{9,10},{10,11},{11... | collective-permute-start | bytes 8847368 | tf_op jit(solution)/shard_map/while/body/eval_jaxpr/ppermute | solution.py:82
  2215.8 31.6 slice-start
  2287.5 13.9 collective-permute-start.2
  2302.3 229.3 %copy-start.21 = (f32[2,12,16]{1,2,0:T(8,128)}, f32[2,12,16]{1,2,0:T(8,128)S(1)}, u32[]{:S(2)}) copy-start(f32[2,12,16]{1,2,0:T(8,128)S(1)} %get-tuple-element.784) | copy-start | bytes 4612 | tf_op jit(solution)/shard_map/while
  2524.8 70.2 %collective-permute-start = (bf16[15,64,2,12,64]{4,1,3,0,2:T(8,128)(2,1)}, bf16[15,64,2,12,64]{4,1,3,0,2:T(8,128)(2,1)}, u32[]{:S(2)}, u32[]{:S(2)}) collective-permute-start(bf16[15,64,2,12,64]{4,1,3,0,2:T(8,128)(2,1)} %copy.173), channel_id=1, source_target_pairs={{0,1},{1,2},{2,3},{3,4},{4,5},{5,6},{6,7},{8,9},{9,10},{10,11},{11... | collective-permute-start | bytes 8847368 | tf_op jit(solution)/shard_map/while/body/eval_jaxpr/ppermute | solution.py:82
  2534.5 95.4 %copy-start.24 = (pred[16,31]{1,0:T(8,128)(4,1)}, pred[16,31]{1,0:T(8,128)(4,1)S(1)}, u32[]{:S(2)}) copy-start(pred[16,31]{1,0:T(8,128)(4,1)S(1)} %get-tuple-element.697) | copy-start | bytes 1492 | tf_op jit(solution)/shard_map/while
  2608.1 31.4 slice-start.2
  2864.5 35.1 copy-start.31
  2868.3 94.9 %collective-permute-start.1 = (bf16[15,64,2,12,64]{4,1,3,0,2:T(8,128)(2,1)}, bf16[15,64,2,12,64]{4,1,3,0,2:T(8,128)(2,1)}, u32[]{:S(2)}, u32[]{:S(2)}) collective-permute-start(bf16[15,64,2,12,64]{4,1,3,0,2:T(8,128)(2,1)} %copy.180), channel_id=1, source_target_pairs={{0,1},{1,2},{2,3},{3,4},{4,5},{5,6},{6,7},{8,9},{9,10},{10,11},{11... | collective-permute-start | bytes 8847368 | tf_op jit(solution)/shard_map/while/body/eval_jaxpr/ppermute | solution.py:82
  2976.4 31.6 slice-start
  3048.0 16.0 collective-permute-start.2
  3064.9 230.7 %copy-start.21 = (f32[2,12,16]{1,2,0:T(8,128)}, f32[2,12,16]{1,2,0:T(8,128)S(1)}, u32[]{:S(2)}) copy-start(f32[2,12,16]{1,2,0:T(8,128)S(1)} %get-tuple-element.784) | copy-start | bytes 4612 | tf_op jit(solution)/shard_map/while
  3283.3 75.8 %collective-permute-start = (bf16[15,64,2,12,64]{4,1,3,0,2:T(8,128)(2,1)}, bf16[15,64,2,12,64]{4,1,3,0,2:T(8,128)(2,1)}, u32[]{:S(2)}, u32[]{:S(2)}) collective-permute-start(bf16[15,64,2,12,64]{4,1,3,0,2:T(8,128)(2,1)} %copy.173), channel_id=1, source_target_pairs={{0,1},{1,2},{2,3},{3,4},{4,5},{5,6},{6,7},{8,9},{9,10},{10,11},{11... | collective-permute-start | bytes 8847368 | tf_op jit(solution)/shard_map/while/body/eval_jaxpr/ppermute | solution.py:82
  3298.6 95.4 %copy-start.24 = (pred[16,31]{1,0:T(8,128)(4,1)}, pred[16,31]{1,0:T(8,128)(4,1)S(1)}, u32[]{:S(2)}) copy-start(pred[16,31]{1,0:T(8,128)(4,1)S(1)} %get-tuple-element.697) | copy-start | bytes 1492 | tf_op jit(solution)/shard_map/while
  3372.2 31.4 slice-start.2
  3628.6 38.0 copy-start.31
  3632.4 97.8 %collective-permute-start.1 = (bf16[15,64,2,12,64]{4,1,3,0,2:T(8,128)(2,1)}, bf16[15,64,2,12,64]{4,1,3,0,2:T(8,128)(2,1)}, u32[]{:S(2)}, u32[]{:S(2)}) collective-permute-start(bf16[15,64,2,12,64]{4,1,3,0,2:T(8,128)(2,1)} %copy.180), channel_id=1, source_target_pairs={{0,1},{1,2},{2,3},{3,4},{4,5},{5,6},{6,7},{8,9},{9,10},{10,11},{11... | collective-permute-start | bytes 8847368 | tf_op jit(solution)/shard_map/while/body/eval_jaxpr/ppermute | solution.py:82
  3743.4 31.6 slice-start
  3815.0 13.9 collective-permute-start.2
  3829.8 229.2 %copy-start.21 = (f32[2,12,16]{1,2,0:T(8,128)}, f32[2,12,16]{1,2,0:T(8,128)S(1)}, u32[]{:S(2)}) copy-start(f32[2,12,16]{1,2,0:T(8,128)S(1)} %get-tuple-element.784) | copy-start | bytes 4612 | tf_op jit(solution)/shard_map/while
  4051.1 71.4 %collective-permute-start = (bf16[15,64,2,12,64]{4,1,3,0,2:T(8,128)(2,1)}, bf16[15,64,2,12,64]{4,1,3,0,2:T(8,128)(2,1)}, u32[]{:S(2)}, u32[]{:S(2)}) collective-permute-start(bf16[15,64,2,12,64]{4,1,3,0,2:T(8,128)(2,1)} %copy.173), channel_id=1, source_target_pairs={{0,1},{1,2},{2,3},{3,4},{4,5},{5,6},{6,7},{8,9},{9,10},{10,11},{11... | collective-permute-start | bytes 8847368 | tf_op jit(solution)/shard_map/while/body/eval_jaxpr/ppermute | solution.py:82
  4062.0 95.4 %copy-start.24 = (pred[16,31]{1,0:T(8,128)(4,1)}, pred[16,31]{1,0:T(8,128)(4,1)S(1)}, u32[]{:S(2)}) copy-start(pred[16,31]{1,0:T(8,128)(4,1)S(1)} %get-tuple-element.697) | copy-start | bytes 1492 | tf_op jit(solution)/shard_map/while
  4135.6 31.4 slice-start.2
  4392.0 36.6 copy-start.31
  4395.9 96.4 %collective-permute-start.1 = (bf16[15,64,2,12,64]{4,1,3,0,2:T(8,128)(2,1)}, bf16[15,64,2,12,64]{4,1,3,0,2:T(8,128)(2,1)}, u32[]{:S(2)}, u32[]{:S(2)}) collective-permute-start(bf16[15,64,2,12,64]{4,1,3,0,2:T(8,128)(2,1)} %copy.180), channel_id=1, source_target_pairs={{0,1},{1,2},{2,3},{3,4},{4,5},{5,6},{6,7},{8,9},{9,10},{10,11},{11... | collective-permute-start | bytes 8847368 | tf_op jit(solution)/shard_map/while/body/eval_jaxpr/ppermute | solution.py:82
  4505.4 31.6 slice-start
  4577.0 14.5 collective-permute-start.2
  (205 other events, 1314.5 us)
where the time goes:
time: 4620 us; the launch traced here: 4590 us
  local copies, waits for them, and re-layouts  1200 us (26%)
  matrix products  1150 us (25%)
  blocking collectives  869 us (19%)
  waiting for transfers between devices  668 us (14%)
  other arithmetic  421 us (9%)
  starting transfers between devices  266 us (6%)
    ppermute x12, waiting for transfers between devices, one_step(): lax.ppermute(qkv_loc[n_frames - window + 1:, :, 1:], 'frames', to_next)  668 us
    all_to_all x12, blocking collectives, spatial_block(): qkv_full = lax.all_to_all(qkv_loc, 'tokens', 3, 1, tiled=True)  563 us
    while x534, local copies, waits for them, and re-layouts  465 us
    all_to_all x24, local copies, waits for them, and re-layouts, spatial_block(): qkv_full = lax.all_to_all(qkv_loc, 'tokens', 3, 1, tiled=True)  353 us
    dot_general x12, matrix products, temporal_attend(): jnp.einsum('aphe,bphe->phab', qkv_loc[:, :, 0], keys_ext, preferred_eleme...  262 us
    ppermute x12, starting transfers between devices, one_step(): lax.ppermute(qkv_loc[n_frames - window + 1:, :, 1:], 'frames', to_next)  254 us
    all_to_all x12, blocking collectives, spatial_block(): attn_loc = lax.all_to_all(attn_out, 'tokens', 1, 2, tiled=True)  236 us
    dot_general x12, matrix products, mlp_block(): jnp.einsum('apk,kd->apd', jax.nn.gelu(hidden, approximate=True).astype(jn...  195 us
  transfers between devices with their start and end apart: 18, of which 12 were waited for; matrix products, arithmetic and copies ran while one was open for 2% of the time, Pallas kernels for 0%

commit v1 on v0

v1 whole, which is shorter than its diff:
```python
import functools

import jax
import jax.numpy as jnp
from jax import lax
from jax.experimental import pallas as pl
from jax.experimental.pallas import tpu as pltpu
from jax.sharding import PartitionSpec as P

MESH = pl.DeviceIdType.MESH
BF = jnp.bfloat16
F32 = jnp.float32
LANES = 128
SUB = 8
CHUNKS = 2


def mm(a, b):
    return jnp.dot(a, b, preferred_element_type=F32)


def mm_t(a, b):
    return lax.dot_general(a, b, (((1,), (1,)), ((), ())), preferred_element_type=F32)


def norm(xv):
    mean = jnp.mean(xv, axis=-1, keepdims=True)
    cen = xv - mean
    var = jnp.mean(cen * cen, axis=-1, keepdims=True)
    return cen * lax.rsqrt(var + 1e-6)


def gelu(hv):
    inner = 0.7978845608028654 * (hv + 0.044715 * (hv * hv * hv))
    return 0.5 * hv * (1.0 + jnp.tanh(inner))


def roles(mesh_tokens, mesh_frames):
    tok, frm = lax.axis_index("tokens"), lax.axis_index("frames")
    chip, core = frm // 2, frm % 2
    odd = (tok // 2 + chip) % 2
    half = ((tok + 1) // 2) % 2
    return tok, frm, chip, core, odd, half


def kernel(cfg, z_in, mod, noise, bias, w_in, w_out, sqkv_h, so_h, tqkv_h, to_h, up_h, down_h, z, emit,
           x, ust, us, kvs, qs, obuf, osnd, ut, utr, qt, kt, vt, sc, pb, bm, ob, uu, hb,
           sqkv, so, tqkv, to, up, down,
           us_s, us_r, o_s, o_r, ut_s, ut_r, w_sem, credit):
    L, S, NC, CH, TK, D, FF, HD, MT, MF, WIN = cfg
    R, HS, RH, G = CH * TK, CH // 2, CH * TK // 2, TK // SUB
    CR = CH * SUB
    SR = NC * CH * SUB
    NT = L * S
    HP = D // LANES
    W = min(256, D)
    DT = D // W
    FT = min(256, FF)
    qscale = HD ** -0.5

    vid = lax.axis_index("videos")
    tok, frm, chip, core, odd, _ = roles(MT, MF)
    sib_f = frm + 1 - 2 * core
    par_t = tok + 1 - 2 * (tok % 2)
    block = chip * 2 + odd
    first = block == 0
    sib = (vid, tok, sib_f)
    par_a = (vid, par_t, frm)
    par_b = (vid, par_t, sib_f)
    nxt = (vid, jnp.where(odd == 0, MT - 1 - tok, tok), jnp.where(odd == 0, frm, (frm + 2) % MF))
    prv = (vid, jnp.where(odd == 1, MT - 1 - tok, tok), jnp.where(odd == 1, frm, (frm + MF - 2) % MF))

    def w_copy(k, layer):
        src, dst = ((sqkv_h, sqkv), (so_h, so), (to_h, to), (up_h, up), (down_h, down))[k]
        return pltpu.make_async_copy(src.at[layer], dst, w_sem.at[k])

    def t_copy(layer):
        return pltpu.make_async_copy(tqkv_h.at[layer], tqkv.at[layer], w_sem.at[5 + layer])

    w_copy(0, 0).start()
    w_copy(1, 0).start()
    for layer in range(L):
        t_copy(layer).start()

    barrier = pltpu.get_barrier_semaphore()
    for dev in (sib, par_a, par_b, nxt, prv):
        pl.semaphore_signal(barrier, inc=1, device_id=dev, device_id_type=MESH)
    pl.semaphore_wait(barrier, 5)

    def remote(src, dst, ss, rs, dev):
        return pltpu.make_async_remote_copy(src_ref=src, dst_ref=dst, send_sem=ss, recv_sem=rs, device_id=dev, device_id_type=MESH)

    def us_copies(par, i):
        return (
            remote(ust.at[i, 1 - core], us.at[par, i, 0], us_s.at[i, 0], us_r.at[par, i, 0], sib),
            remote(ust.at[i, core], us.at[par, i, 1], us_s.at[i, 1], us_r.at[par, i, 1], par_a),
            remote(ust.at[i, 1 - core], us.at[par, i, 2], us_s.at[i, 2], us_r.at[par, i, 2], par_b),
        )

    def o_copy(i):
        return remote(osnd.at[i], obuf.at[i, core], o_s.at[i], o_r.at[i], sib)

    def ut_copy(par, i):
        return remote(ut.at[i], utr.at[par, i], ut_s.at[i], ut_r.at[par, i], nxt)

    z[...] = z_in[...]
    emit[...] = jnp.zeros_like(emit)
    for g in range(G):
        for ref in (kt, vt):
            ref[g] = jnp.zeros(ref.shape[1:], BF)

    lane = lax.broadcasted_iota(jnp.int32, (1, LANES), 1)
    low = lane < HD

    def stack_heads(q):
        zero = jnp.zeros_like(q)
        return jnp.concatenate([jnp.where(low, q, zero), jnp.where(low, zero, q)], axis=0)

    def softmax_rows(sv):
        top = jnp.max(sv, axis=-1, keepdims=True)
        e = jnp.exp(sv - top)
        return (e * (1.0 / jnp.sum(e, axis=-1, keepdims=True))).astype(BF)

    def modulated(i, a, layer, step, which):
        row = i * CH + a + (S - 1) - step
        shift = mod[row, pl.ds(layer * 6 + 2 * which, 1), :]
        scale = mod[row, pl.ds(layer * 6 + 2 * which + 1, 1), :]
        xv = x[i, pl.ds(a * TK, TK), :]
        return (norm(xv) * (1.0 + scale) + shift).astype(BF)

    def spatial(i, par):
        for c in us_copies(par, i):
            c.wait()
        own = ust[i, core]
        u_all = jnp.concatenate([own, us[par, i, 0], us[par, i, 1], us[par, i, 2]], axis=0)
        u_q = jnp.concatenate([own, us[par, i, 0]], axis=0)
        for t in range(DT):
            y = (mm(u_q, sqkv[:, t * W:(t + 1) * W]) * qscale).astype(BF)
            for p in range(2):
                for s in range(HS):
                    qs[s, p * TK:(p + 1) * TK, t * W:(t + 1) * W] = y[p * RH + s * TK:p * RH + (s + 1) * TK]
        for t in range(2 * DT):
            y = mm(u_all, sqkv[:, D + t * W:D + (t + 1) * W]).astype(BF)
            for p in range(4):
                for s in range(HS):
                    kvs[s, p * TK:(p + 1) * TK, t * W:(t + 1) * W] = y[p * RH + s * TK:p * RH + (s + 1) * TK]

        @pl.loop(0, HS)
        def _(s):
            for h in range(HP):
                cols = slice(h * LANES, (h + 1) * LANES)
                sc[h, 0:4 * TK, 0:4 * TK] = mm_t(stack_heads(qs[s, :, cols]), kvs[s, :, cols])
            for h in range(HP):
                pb[h, 0:4 * TK, 0:4 * TK] = softmax_rows(sc[h, 0:4 * TK, 0:4 * TK])
            for h in range(HP):
                cols = slice(h * LANES, (h + 1) * LANES)
                o2 = mm(pb[h, 0:4 * TK, 0:4 * TK], kvs[s, :, D + h * LANES:D + (h + 1) * LANES])
                o = jnp.where(low, o2[:2 * TK], o2[2 * TK:]).astype(BF)
                rows = pl.ds(pl.multiple_of(s * TK, TK), TK)
                obuf[i, core, rows, cols] = o[:TK]
                osnd[i, rows, cols] = o[TK:]

        o_copy(i).start()

    def project(i, par, layer, step, n):
        o_copy(i).wait()
        ov = obuf[i].reshape(R, D)
        for t in range(DT):
            cols = slice(t * W, (t + 1) * W)
            x[i, :, cols] = x[i, :, cols] + mm(ov, so[:, cols])
        for a in range(CH):
            ut[i, a * TK:(a + 1) * TK, :] = modulated(i, a, layer, step, 1)

        @pl.when((i == NC - 1) & (n >= 2))
        def _():
            pl.semaphore_wait(credit, 1)

        ut_copy(par, i).start()
        uv = ut[i]
        for t in range(3 * DT):
            y = mm(uv, tqkv[layer, :, t * W:(t + 1) * W])
            kind, tt = t // DT, t % DT
            if kind == 0:
                y = y * qscale
            y4 = y.reshape(CH, G, SUB, W)
            for g in range(G):
                yg = y4[:, g].reshape(CR, W).astype(BF)
                if kind == 0:
                    qt[g, pl.ds(pl.multiple_of(i * CR, CR), CR), tt * W:(tt + 1) * W] = yg
                else:
                    ref = kt if kind == 1 else vt
                    ref[g, pl.ds(pl.multiple_of(SR + i * CR, CR), CR), tt * W:(tt + 1) * W] = yg

    def temporal(i, par, layer, step):
        ut_copy(par, i).wait()
        uv = utr[par, i]
        for t in range(2 * DT):
            y = mm(uv, tqkv[layer, :, D + t * W:D + (t + 1) * W])
            kind, tt = t // DT, t % DT
            ref = vt if kind else kt
            y4 = y.reshape(CH, G, SUB, W)
            for g in range(G):
                ref[g, pl.ds(pl.multiple_of(i * CR, CR), CR), tt * W:(tt + 1) * W] = y4[:, g].reshape(CR, W).astype(BF)
        rows = lax.broadcasted_iota(jnp.int32, (2 * CR, WIN), 0)
        keys = lax.broadcasted_iota(jnp.int32, (2 * CR, WIN), 1)
        pos_q = i * CH + (rows & (CR - 1)) // SUB
        pos_k = (i - NC) * CH + keys // SUB
        pos = block * NC * CH + pos_q - step
        slot = jnp.where(pos < 0, pos + MF * NC * CH, pos)
        valid = pos_q - pos_k <= slot
        for h in range(HP):
            bm[h] = jnp.where(valid, bias[layer, h], -jnp.inf)

        @pl.loop(0, G // 2)
        def _(gg):
            qrows = pl.ds(pl.multiple_of(i * CR, CR), CR)
            krows = pl.ds(pl.multiple_of(i * CR, CR), WIN)
            units = [(gg * 2 + d, d * 2 * CR, h) for d in range(2) for h in range(HP)]
            for g, r, h in units:
                cols = slice(h * LANES, (h + 1) * LANES)
                sc[h, r:r + 2 * CR, 0:WIN] = mm_t(stack_heads(qt[g, qrows, cols]), kt[g, krows, cols]) + bm[h]
            for g, r, h in units:
                pb[h, r:r + 2 * CR, 0:WIN] = softmax_rows(sc[h, r:r + 2 * CR, 0:WIN])
            for g, r, h in units:
                cols = slice(h * LANES, (h + 1) * LANES)
                o2 = mm(pb[h, r:r + 2 * CR, 0:WIN], vt[g, krows, cols])
                ob[pl.ds(pl.multiple_of(g * CR, CR), CR), cols] = jnp.where(low, o2[:CR], o2[CR:]).astype(BF)

        ov = ob[...]
        for t in range(DT):
            cols = slice(t * W, (t + 1) * W)
            y4 = mm(ov, to[:, cols]).reshape(G, CH, SUB, W)
            for a in range(CH):
                x[i, a * TK:(a + 1) * TK, cols] = x[i, a * TK:(a + 1) * TK, cols] + y4[:, a].reshape(TK, W)

    def mlp(i, layer, step):
        for a in range(CH):
            uu[a * TK:(a + 1) * TK, :] = modulated(i, a, layer, step, 2)
        uv = uu[...]
        for t in range(FF // FT):
            hp = mm(uv, up[:, t * FT:(t + 1) * FT])
            for r in range(0, R, 128):
                hb[r:r + 128, t * FT:(t + 1) * FT] = gelu(hp[r:r + 128]).astype(BF)
        for t in range(DT):
            cols = slice(t * W, (t + 1) * W)
            for r in range(0, R, 256):
                x[i, r:r + 256, cols] = x[i, r:r + 256, cols] + mm(hb[r:r + 256], down[:, cols])

    def finish(i, step):
        for a in range(CH):
            uu[a * TK:(a + 1) * TK, :] = norm(x[i, a * TK:(a + 1) * TK, :]).astype(BF)
        v = mm(uu[...], w_out[...])
        for a in range(CH):
            row = i * CH + a + (S - 1) - step
            dt = mod[row, pl.ds(6 * L, 1), 0:LANES]
            z[i, a * TK:(a + 1) * TK, :] = z[i, a * TK:(a + 1) * TK, :] + dt * v[a * TK:(a + 1) * TK]

        @pl.when(i == step // CH)
        def _():
            rows = pl.ds(pl.multiple_of((step % CH) * TK, TK), TK)
            zv = z[i, rows, :]
            emit[step] = zv
            z[i, rows, :] = jnp.where(first, noise[step], zv)

    def enter(i):
        x[i] = mm(z[i].astype(BF), w_in[...]).astype(BF).astype(F32)

    def launch(i, par, layer, step):
        for a in range(CH):
            ust[i, a // HS, (a % HS) * TK:(a % HS + 1) * TK, :] = modulated(i, a, layer, step, 0)
        for c in us_copies(par, i):
            c.start()

    @pl.loop(0, NT + 1)
    def _(m):
        n = m - 1
        layer, step, par = lax.rem(n + L, L), (n + L) // L - 1, lax.rem(n + 2, 2)
        nlayer, nstep, npar = lax.rem(m, L), m // L, lax.rem(m, 2)

        @pl.when(m > 0)
        def _():
            w_copy(0, layer).wait()
            w_copy(1, layer).wait()

            @pl.when(m == 1)
            def _():
                for q in range(L):
                    t_copy(q).wait()

            for k in (2, 3, 4):
                w_copy(k, layer).start()

            @pl.loop(0, NC)
            def _(c):
                spatial(NC - 1 - c, par)
                project(NC - 1 - c, par, layer, step, n)

            for k in (2, 3, 4):
                w_copy(k, layer).wait()

            @pl.when(m < NT)
            def _():
                w_copy(0, nlayer).start()
                w_copy(1, nlayer).start()

        @pl.loop(0, NC)
        def _(c):
            i = NC - 1 - c

            @pl.when(m > 0)
            def _():
                temporal(i, par, layer, step)
                mlp(i, layer, step)

                @pl.when(layer == L - 1)
                def _():
                    finish(i, step)

            @pl.when(m < NT)
            def _():
                @pl.when(nlayer == 0)
                def _():
                    enter(i)

                launch(i, npar, nlayer, nstep)

        @pl.when(m > 0)
        def _():
            pl.semaphore_signal(credit, inc=1, device_id=prv, device_id_type=MESH)

    pl.semaphore_wait(credit, min(2, NT))


def denoise_call(cfg, vmem, *args):
    L, S, NC, CH, TK, D, FF, HD, MT, MF, WIN = cfg
    R, HS, RH, G = CH * TK, CH // 2, CH * TK // 2, TK // SUB
    CR, SR = CH * SUB, NC * CH * SUB
    HP = D // LANES
    KR = (NC - 1) * CR + WIN
    scr = [
        pltpu.VMEM((NC, R, D), F32),
        pltpu.VMEM((NC, 2, RH, D), BF),
        pltpu.VMEM((2, NC, 3, RH, D), BF),
        pltpu.VMEM((HS, 4 * TK, 2 * D), BF),
        pltpu.VMEM((HS, 2 * TK, D), BF),
        pltpu.VMEM((NC, 2, RH, D), BF),
        pltpu.VMEM((NC, RH, D), BF),
        pltpu.VMEM((NC, R, D), BF),
        pltpu.VMEM((2, NC, R, D), BF),
        pltpu.VMEM((G, SR, D), BF),
        pltpu.VMEM((G, KR, D), BF),
        pltpu.VMEM((G, KR, D), BF),
        pltpu.VMEM((HP, max(4 * TK, 4 * CR), max(4 * TK, WIN)), F32),
        pltpu.VMEM((HP, max(4 * TK, 4 * CR), max(4 * TK, WIN)), BF),
        pltpu.VMEM((HP, 2 * CR, WIN), F32),
        pltpu.VMEM((R, D), BF),
        pltpu.VMEM((R, D), BF),
        pltpu.VMEM((R, FF), BF),
        pltpu.VMEM((D, 3 * D), BF),
        pltpu.VMEM((D, D), BF),
        pltpu.VMEM((L, D, 3 * D), BF),
        pltpu.VMEM((D, D), BF),
        pltpu.VMEM((D, FF), BF),
        pltpu.VMEM((FF, D), BF),
        pltpu.SemaphoreType.DMA((NC, 3)),
        pltpu.SemaphoreType.DMA((2, NC, 3)),
        pltpu.SemaphoreType.DMA((NC,)),
        pltpu.SemaphoreType.DMA((NC,)),
        pltpu.SemaphoreType.DMA((NC,)),
        pltpu.SemaphoreType.DMA((2, NC)),
        pltpu.SemaphoreType.DMA((5 + L,)),
        pltpu.SemaphoreType.REGULAR,
    ]
    inner = pl.BlockSpec(memory_space=pltpu.VMEM)
    outer = pl.BlockSpec(memory_space=pl.ANY)
    return pl.pallas_call(
        functools.partial(kernel, cfg),
        out_shape=(jax.ShapeDtypeStruct((NC, R, LANES), F32), jax.ShapeDtypeStruct((S, TK, LANES), F32)),
        in_specs=[inner] * 6 + [outer] * 6,
        out_specs=(inner, inner),
        scratch_shapes=scr,
        compiler_params=pltpu.CompilerParams(collective_id=0, has_side_effects=True, vmem_limit_bytes=vmem),
        name="fifo_denoise",
    )(*args)


def lag_bias_tiles(lag_bias, CH, SLOTS, WIN):
    L, H, window = lag_bias.shape
    a = jnp.arange(CH)[:, None, None, None]
    tq = jnp.arange(SUB)[None, :, None, None]
    k = jnp.arange(WIN // SUB)[None, None, :, None]
    tk = jnp.arange(SUB)[None, None, None, :]
    lag = SLOTS + a - k
    ok = (lag >= 0) & (lag < window) & (tq == tk)
    tiles = jnp.where(ok, jnp.take(lag_bias, jnp.clip(lag, 0, window - 1), axis=2), -jnp.inf)
    return tiles.reshape(L, H // 2, 2 * CH * SUB, WIN)


def solution(mesh):
    MT, MF = mesh.shape["tokens"], mesh.shape["frames"]
    slot_spec = P(("videos", "frames"), "tokens", None)
    mod_spec = P(("videos", "frames"), None, None, None)
    step_spec = P(("videos", "frames"))
    noise_spec = P("videos", "tokens", None)
    emit_spec = P("videos", ("tokens", "frames"), None)
    to_sib = [(f, f ^ 1) for f in range(MF)]
    to_next_chip = [(f, (f + 2) % MF) for f in range(MF)]

    def body(z_loc, mod_loc, step_loc, noise_loc, lag_bias, w_in, w_out, w_sqkv, w_so, w_tqkv, w_to, w_up, w_down):
        SL, TK, C = z_loc.shape
        S = noise_loc.shape[0]
        L, D, FF = w_up.shape
        HD = w_so.shape[2]
        NC = CHUNKS
        CH = SL // NC
        WIN = 2 * SL * SUB
        tok, frm, chip, core, odd, half = roles(MT, MF)
        quarter = 2 * half + core

        zn = jnp.concatenate([z_loc.reshape(SL, TK * C), noise_loc.reshape(S, TK * C)], axis=0)
        zn = lax.all_gather(zn, "tokens", axis=0)
        zq = lax.dynamic_index_in_dim(zn, quarter, axis=0, keepdims=False)
        sent = lax.dynamic_index_in_dim(zn, 2 * half + (1 - core), axis=0, keepdims=False)[:SL]
        z_sib = lax.ppermute(sent, "frames", to_sib)
        z_own = jnp.where(odd == core, zq[:SL], z_sib).reshape(SL, TK, C)
        noise = zq[SL:].reshape(S, TK, C)
        pad = lambda v: jnp.pad(v, ((0, 0),) * (v.ndim - 1) + ((0, LANES - C),))

        table = jnp.concatenate([mod_loc.reshape(SL, L * 6, D), jnp.broadcast_to(step_loc[:, None, None], (SL, 1, D))], axis=1)
        table_sib = lax.ppermute(table, "frames", to_sib)
        even_blk = jnp.where(core == 0, table, table_sib)
        odd_blk = jnp.where(core == 1, table, table_sib)
        tail = lax.ppermute(odd_blk[SL - (S - 1):], "frames", to_next_chip)
        own_tab = jnp.where(odd == 0, even_blk, odd_blk)
        prev_tab = jnp.where(odd == 0, tail, even_blk[SL - (S - 1):])
        mod = jnp.concatenate([prev_tab, own_tab], axis=0)

        cfg = (L, S, NC, CH, TK, D, FF, HD, MT, MF, WIN)
        z_new, emit = denoise_call(
            cfg, 67043328,
            pad(z_own).reshape(NC, CH * TK, LANES), mod, pad(noise), lag_bias_tiles(lag_bias, CH, SL, WIN),
            jnp.pad(w_in, ((0, LANES - C), (0, 0))), jnp.pad(w_out, ((0, 0), (0, LANES - C))),
            w_sqkv.reshape(L, D, 3 * D), w_so.reshape(L, D, D), w_tqkv.reshape(L, D, 3 * D), w_to.reshape(L, D, D), w_up, w_down,
        )

        mine = jnp.concatenate([z_new.reshape(SL, TK, LANES)[:, :, :C].reshape(SL, TK * C), emit[:, :, :C].reshape(S, TK * C)], axis=0)
        every = lax.all_gather(mine, ("tokens", "frames"), axis=0)
        where_is = []
        for blk in range(MF):
            for q in range(MT):
                xx, o, hf, cc = blk // 2, blk % 2, q // 2, q % 2
                ty = [t for t in range(MT) if (t // 2 + xx) % 2 == o and ((t + 1) // 2) % 2 == hf]
                where_is.append(ty[0] * MF + 2 * xx + cc)
        queue = jnp.stack([every[d, :SL] for d in where_is]).reshape(MF, MT, SL, TK * C)
        queue = jnp.roll(jnp.swapaxes(queue, 1, 2).reshape(MF * SL, MT, TK * C), -S, axis=0)
        z_fin = lax.dynamic_slice(queue, (frm * SL, tok, 0), (SL, 1, TK * C)).reshape(SL, TK, C)
        em = jnp.stack([every[where_is[q], SL:] for q in range(MT)])
        per = TK // MF
        em = lax.dynamic_slice(em, (tok, 0, frm * per * C), (1, S, per * C)).reshape(S, per, C)
        return em, z_fin

    return jax.shard_map(body, mesh=mesh, in_specs=(slot_spec, mod_spec, step_spec, noise_spec) + (P(),) * 9, out_specs=(emit_spec, slot_spec), check_vma=False)
```

time: 4620 us -> 878 us (0.19)
  matrix products: 1150 us -> 0 us
  local copies, waits for them, and re-layouts: 1200 us -> 76.9 us
  blocking collectives: 869 us -> 37.9 us
  Pallas kernels: 0 us -> 739 us
  waiting for transfers between devices: 668 us -> 5.54 us
  other arithmetic: 421 us -> 5.65 us
  starting transfers between devices: 266 us -> 6.21 us
    dot_general x120 -> x0, matrix products: 1150 us -> none  [the longest x12 262 us: temporal_attend(): jnp.einsum('aphe,bphe->phab', qkv_loc[:, :, 0], keys_ext, preferred_eleme...]
    all_to_all x24 -> x0, blocking collectives: 799 us -> none  [the longest x12 563 us: spatial_block(): qkv_full = lax.all_to_all(qkv_loc, 'tokens', 3, 1, tiled=True)]
    pallas_call x0 -> x1, Pallas kernels: none -> 739 us  [denoise_call(): pl.pallas_call(functools.partial(kernel, cfg), out_shape=(jax.ShapeDtypeS...]
    ppermute x18 -> x3, waiting for transfers between devices: 668 us -> 5.54 us  [the longest x1 5.54 us: body(): tail = lax.ppermute(odd_blk[SL - (S - 1):], 'frames', to_next_chip)]
    while x536 -> x0, local copies, waits for them, and re-layouts: 468 us -> none
    all_to_all x36 -> x0, local copies, waits for them, and re-layouts: 363 us -> none  [the longest x24 353 us: spatial_block(): qkv_full = lax.all_to_all(qkv_loc, 'tokens', 3, 1, tiled=True)]
    sub x30 -> x0, other arithmetic: 306 us -> none  [the longest x12 190 us: spatial_block(): attn_prob = jax.nn.softmax(scores, axis=-1).astype(jnp.bfloat16)]
    ppermute x18 -> x3, starting transfers between devices: 266 us -> 6.21 us  [the longest x1 2.75 us: body(): z_sib = lax.ppermute(sent, 'frames', to_sib)]
  transfers between devices with their start and end apart: 18 -> 3, of which waited for: 12 -> 1; matrix products, arithmetic and copies ran while one was open for 2% -> 8% of each run, Pallas kernels for 0% -> 0%
where the time goes in v1:
time: 878 us; the launch traced here: 872 us
  Pallas kernels  739 us (84%)
  local copies, waits for them, and re-layouts  76.9 us (9%)
  blocking collectives  37.9 us (4%)
    pallas_call x1, Pallas kernels, denoise_call(): pl.pallas_call(functools.partial(kernel, cfg), out_shape=(jax.ShapeDtypeS...  739 us
    broadcast_in_dim x4, local copies, waits for them, and re-layouts, lag_bias_tiles(): jnp.where(ok, jnp.take(lag_bias, jnp.clip(lag, 0, window - 1), axis=2), -...  41.2 us
    all_gather x1, blocking collectives, body(): every = lax.all_gather(mine, ('tokens', 'frames'), axis=0)  27.7 us
  transfers between devices with their start and end apart: 3, of which 1 were waited for; matrix products, arithmetic and copies ran while one was open for 8% of the time, Pallas kernels for 0%

profile of v1, /device:TPU:97, one launch (start us, length us, event | category | flops | bytes accessed | tf_op | source)
XLA Modules:
  0.0 871.9 jit_solution(11475203794430401161)
XLA Ops:
  0.6 1.2 copy.66
  1.9 0.4 copy.67
  2.2 0.8 broadcast_in_dim.42
  3.0 0.1 copy-done
  3.1 0.1 pad_maximum_fusion.1
  3.2 1.2 copy.68
  4.5 2.0 collective-permute-start.1
  6.5 0.1 copy.62
  6.6 0.1 reshape.200
  6.8 0.1 copy.61
  7.0 10.2 %all-gather.2 = f32[4,22,256]{2,1,0:T(8,128)S(1)} all-gather(f32[1,22,256]{2,1,0:T(8,128)S(1)} %maximum_bitcast_fusion), channel_id=2, replica_groups=mesh['videos'=1,'tokens'=4,'frames'=8] {'tokens'}, dimensions={0}, use_global_device_ids=true | all-gather | bytes 112640 | tf_op jit(solution)/shard_map/all_gather | solution.py:421
  17.2 0.6 dynamic-slice_bitcast_fusion
  17.8 2.7 collective-permute-start
  20.6 0.1 fusion.7
  20.7 0.2 reshape.204
  20.9 0.1 reshape.218
  21.0 0.1 copy.71
  21.1 1.0 gather_fusion
  22.1 0.3 select_bitcast_fusion
  22.5 0.2 copy.72
  22.6 11.6 %broadcast_in_dim.48 = f32[2,12,8,8,32,8]{5,4,3,2,1,0:T(8,128)} broadcast(f32[2,12,8,32]{3,2,1,0:T(8,128)S(1)} %copy.72), dimensions={0,1,2,4} | broadcast | bytes 1597440 | tf_op jit(solution)/shard_map/jit(_where)/broadcast_in_dim | solution.py:395
  34.2 19.4 %broadcast_in_dim.49 = f32[2,6,128,256]{3,2,1,0:T(8,128)} reshape(f32[2,12,8,8,32,8]{5,4,3,2,1,0:T(8,128)} %broadcast_in_dim.48) | data formatting | bytes 3145728 | tf_op jit(solution)/shard_map/jit(_where)/broadcast_in_dim | solution.py:395
  53.6 0.2 broadcast_and_fusion
  53.8 1.5 broadcast_in_dim.43
  55.4 8.7 broadcast_in_dim.44
  64.0 10.5 %copy.74.sqkv_h = bf16[2,768,2304]{2,1,0:T(8,128)(2,1)} copy(bf16[2,768,2304]{1,2,0:T(8,128)(2,1)} %bitcast.38) | data formatting | bytes 14155776 | tf_op jit(solution)/shard_map/reshape | solution.py:443
  74.5 10.6 %copy.75.tqkv_h = bf16[2,768,2304]{2,1,0:T(8,128)(2,1)} copy(bf16[2,768,2304]{1,2,0:T(8,128)(2,1)} %bitcast.39) | data formatting | bytes 14155776 | tf_op jit(solution)/shard_map/reshape | solution.py:443
  85.2 0.2 copy.73
  85.4 0.7 pad.19.w_out
  86.1 0.7 pad.18.w_in
  86.8 0.7 pad.17.noise
  87.5 1.4 broadcast_select_fusion.bias
  88.8 1.6 broadcast_select_fusion.1
  90.4 1.4 collective-permute-start.2
  91.9 0.7 fusion.1
  92.6 0.1 copy.64
  92.7 0.6 copy.85
  93.3 0.8 pad.16.clone
  94.1 5.5 collective-permute-done.2
  99.7 1.1 pad_maximum_fusion.mod
  100.8 738.7 %fifo_denoise.1 = (f32[2,512,128]{2,1,0:T(8,128)}, f32[6,64,128]{2,1,0:T(8,128)}) custom-call(f32[2,512,128]{2,1,0:T(8,128)} %bitcast.45, f32[21,13,768]{2,1,0:T(8,128)} %pad_maximum_fusion.mod, f32[6,64,128]{2,1,0:T(8,128)} %pad.17.noise, f32[2,6,128,256]{3,2,1,0:T(8,128)} %broadcast_select_fusion.bias, bf16[128,768]{1,0:T(8,128)(2,1)} %pad.18.w_in, ...), custom_call_target="tpu_custom_call" | custom-call | tf_op jit(solution)/shard_map/fifo_denoise/pallas_call | solution.py:376
  839.5 1.5 copy.84
  841.1 1.1 reshape.211
  842.2 27.7 %all-gather.3 = f32[32,22,256]{2,1,0:T(8,128)S(1)} all-gather(f32[1,22,256]{2,1,0:T(8,128)S(1)} %maximum_bitcast_fusion.1), channel_id=3, replica_groups=mesh['videos'=1,'tokens'=4,'frames'=8] {'tokens','frames'}, dimensions={0}, use_global_device_ids=true | all-gather | bytes 743424 | tf_op jit(solution)/shard_map/all_gather | solution.py:447
  870.2 0.1 copy.81
  870.3 0.7 copy.83
  871.0 0.1 fusion.9
  871.2 0.7 copy.82
  (58 shorter events, 0.6 us)
Async XLA Ops:
  0.6 5.9 copy-start.7
  0.6 6.1 copy-start.6
  1.8 19.2 %copy-start.8 = (f32[2,12,16]{2,0,1:T(2,128)S(1)}, f32[2,12,16]{2,0,1:T(2,128)}, u32[]{:S(2)}) copy-start(f32[2,12,16]{2,0,1:T(2,128)} %param.17) | copy-start | bytes 4612
  2.2 0.9 copy-start
  3.1 1.3 copy-start.3
  4.5 84.4 %collective-permute-start.1 = (f32[16,13,768]{2,0,1:T(8,128)}, f32[16,13,768]{2,0,1:T(8,128)}, u32[]{:S(2)}, u32[]{:S(2)}) collective-permute-start(f32[16,13,768]{2,0,1:T(8,128)} %copy.68), channel_id=1, source_target_pairs={{0,1},{1,0},{2,3},{3,2},{4,5},{5,4},{6,7},{7,6},{8,9},{9,8},{10,11... | collective-permute-start | bytes 1916936 | tf_op jit(solution)/shard_map/ppermute | solution.py:430
  17.2 3.6 copy-start.5
  17.8 74.0 %collective-permute-start = (f32[16,256]{1,0:T(8,128)}, f32[16,256]{1,0:T(8,128)S(1)}, u32[]{:S(2)}, u32[]{:S(2)}) collective-permute-start(f32[16,256]{1,0:T(8,128)} %dynamic-slice_bitcast_fusion), channel_id=1, source_target_pairs={{0,1},{1,0},{2,3},{3,2},{4,5},{5,4},{6,7},{7,6},{8,9},{9,8},{10,11... | collective-permute-start | bytes 49160 | tf_op jit(solution)/shard_map/ppermute | solution.py:424
  74.5 10.7 %copy-start.9 = (bf16[768,4]{0,1:T(4,128)(2,1)S(1)}, bf16[768,4]{0,1:T(4,128)(2,1)}, u32[]{:S(2)}) copy-start(bf16[768,4]{0,1:T(4,128)(2,1)} %param.19) | copy-start | bytes 18436
  74.5 11.6 %copy-start.10 = (bf16[4,768]{1,0:T(4,128)(2,1)S(1)}, bf16[4,768]{1,0:T(4,128)(2,1)}, u32[]{:S(2)}) copy-start(bf16[4,768]{1,0:T(4,128)(2,1)} %param.18) | copy-start | bytes 18436
  74.5 13.0 %copy-start.2 = (f32[2,6,128,256]{3,2,1,0:T(8,128)S(1)}, f32[2,6,128,256]{3,2,1,0:T(8,128)}, u32[]{:S(2)}) copy-start(f32[2,6,128,256]{3,2,1,0:T(8,128)} %broadcast_in_dim.49) | copy-start | bytes 4718596
  85.2 3.7 copy-start.1
  85.2 3.7 copy-start.4
  90.4 9.3 %collective-permute-start.2 = (f32[5,13,768]{2,1,0:T(8,128)S(1)}, f32[5,13,768]{2,1,0:T(8,128)S(1)}, u32[]{:S(2)}, u32[]{:S(2)}) collective-permute-start(f32[5,13,768]{2,1,0:T(8,128)S(1)} %slice.157), channel_id=1, source_target_pairs={{0,2},{1,3},{2,4},{3,5},{4,6},{5,7},{6,0},{7,1},{8,10},{9,11},{10,... | collective-permute-start | bytes 599048 | tf_op jit(solution)/shard_map/ppermute | solution.py:433

commit v2 on v1

--- a/solution.py
+++ b/solution.py
@@ -12,7 +12,7 @@
 F32 = jnp.float32
 LANES = 128
 SUB = 8
-CHUNKS = 2
+CHUNKS = 4
 
 
 def mm(a, b):
@@ -43,10 +43,10 @@
     return tok, frm, chip, core, odd, half
 
 
-def kernel(cfg, z_in, mod, noise, bias, w_in, w_out, sqkv_h, so_h, tqkv_h, to_h, up_h, down_h, z, emit,
-           x, ust, us, kvs, qs, obuf, osnd, ut, utr, qt, kt, vt, sc, pb, bm, ob, uu, hb,
+def kernel(cfg, lag_bias, z_in, noise, w_in, w_out, own_tab, prev_tab, sqkv_h, so_h, tqkv_h, to_h, up_h, down_h, z, emit,
+           mod, bias, x, ust, us, kvs, qs, obuf, osnd, ut, utr, qt, kt, vt, pb, bm, ob, uu, hb,
            sqkv, so, tqkv, to, up, down,
-           us_s, us_r, o_s, o_r, ut_s, ut_r, w_sem, credit):
+           us_s, us_r, o_s, o_r, ut_s, ut_r, w_sem, t_sem, credit):
     L, S, NC, CH, TK, D, FF, HD, MT, MF, WIN = cfg
     R, HS, RH, G = CH * TK, CH // 2, CH * TK // 2, TK // SUB
     CR = CH * SUB
@@ -57,6 +57,7 @@
     DT = D // W
     FT = min(256, FF)
     qscale = HD ** -0.5
+    SU, TU, RS = min(2, HS), min(4, G), min(64, 4 * TK)
 
     vid = lax.axis_index("videos")
     tok, frm, chip, core, odd, _ = roles(MT, MF)
@@ -77,6 +78,12 @@
     def t_copy(layer):
         return pltpu.make_async_copy(tqkv_h.at[layer], tqkv.at[layer], w_sem.at[5 + layer])
 
+    tables = (
+        pltpu.make_async_copy(prev_tab, mod.at[0:S - 1], t_sem.at[0]),
+        pltpu.make_async_copy(own_tab, mod.at[S - 1:S - 1 + NC * CH], t_sem.at[1]),
+    )
+    for c in tables:
+        c.start()
     w_copy(0, 0).start()
     w_copy(1, 0).start()
     for layer in range(L):
@@ -109,6 +116,22 @@
         for ref in (kt, vt):
             ref[g] = jnp.zeros(ref.shape[1:], BF)
 
+    q_row = lax.broadcasted_iota(jnp.int32, (CR, WIN), 0)
+    k_col = lax.broadcasted_iota(jnp.int32, (CR, WIN), 1)
+    lag = NC * CH + q_row // SUB - k_col // SUB
+    lag = jnp.where((q_row & (SUB - 1)) == (k_col & (SUB - 1)), lag, -1)
+
+    @pl.loop(0, L * HP)
+    def _(lh):
+        for hd in range(2):
+            tile = jnp.full((CR, WIN), -jnp.inf, F32)
+            for r in range(lag_bias.shape[1]):
+                tile = jnp.where(lag == r, lag_bias[2 * lh + hd, r], tile)
+            bias[lh // HP, lh % HP, hd * CR:(hd + 1) * CR, :] = tile
+
+    for c in tables:
+        c.wait()
+
     lane = lax.broadcasted_iota(jnp.int32, (1, LANES), 1)
     low = lane < HD
 
@@ -121,12 +144,15 @@
         e = jnp.exp(sv - top)
         return (e * (1.0 / jnp.sum(e, axis=-1, keepdims=True))).astype(BF)
 
-    def modulated(i, a, layer, step, which):
+    NR = min(32, TK)
+
+    def modulated(i, a, layer, step, which, put):
         row = i * CH + a + (S - 1) - step
-        shift = mod[row, pl.ds(layer * 6 + 2 * which, 1), :]
-        scale = mod[row, pl.ds(layer * 6 + 2 * which + 1, 1), :]
-        xv = x[i, pl.ds(a * TK, TK), :]
-        return (norm(xv) * (1.0 + scale) + shift).astype(BF)
+        shift = mod[row, pl.ds(2 * which * L + layer, 1), :]
+        gain = 1.0 + mod[row, pl.ds((2 * which + 1) * L + layer, 1), :]
+        for r in range(0, TK, NR):
+            xv = x[i, a * TK + r:a * TK + r + NR, :]
+            put(r, (norm(xv) * gain + shift).astype(BF))
 
     def spatial(i, par):
         for c in us_copies(par, i):
@@ -135,26 +161,27 @@
         u_all = jnp.concatenate([own, us[par, i, 0], us[par, i, 1], us[par, i, 2]], axis=0)
         u_q = jnp.concatenate([own, us[par, i, 0]], axis=0)
         for t in range(DT):
-            y = (mm(u_q, sqkv[:, t * W:(t + 1) * W]) * qscale).astype(BF)
+            y = (mm_t(u_q, sqkv[t * W:(t + 1) * W, :]) * qscale).astype(BF)
             for p in range(2):
                 for s in range(HS):
                     qs[s, p * TK:(p + 1) * TK, t * W:(t + 1) * W] = y[p * RH + s * TK:p * RH + (s + 1) * TK]
         for t in range(2 * DT):
-            y = mm(u_all, sqkv[:, D + t * W:D + (t + 1) * W]).astype(BF)
+            y = mm_t(u_all, sqkv[D + t * W:D + (t + 1) * W, :]).astype(BF)
             for p in range(4):
                 for s in range(HS):
                     kvs[s, p * TK:(p + 1) * TK, t * W:(t + 1) * W] = y[p * RH + s * TK:p * RH + (s + 1) * TK]
 
-        @pl.loop(0, HS)
-        def _(s):
-            for h in range(HP):
+        @pl.loop(0, HS // SU)
+        def _(ss):
+            units = [(ss * SU + d, d * HP + h, h) for d in range(SU) for h in range(HP)]
+            for s, p, h in units:
                 cols = slice(h * LANES, (h + 1) * LANES)
-                sc[h, 0:4 * TK, 0:4 * TK] = mm_t(stack_heads(qs[s, :, cols]), kvs[s, :, cols])
-            for h in range(HP):
-                pb[h, 0:4 * TK, 0:4 * TK] = softmax_rows(sc[h, 0:4 * TK, 0:4 * TK])
-            for h in range(HP):
+                sv = mm_t(stack_heads(qs[s, :, cols]), kvs[s, :, cols])
+                for r in range(0, 4 * TK, RS):
+                    pb[p, r:r + RS, 0:4 * TK] = softmax_rows(sv[r:r + RS])
+            for s, p, h in units:
                 cols = slice(h * LANES, (h + 1) * LANES)
-                o2 = mm(pb[h, 0:4 * TK, 0:4 * TK], kvs[s, :, D + h * LANES:D + (h + 1) * LANES])
+                o2 = mm(pb[p, 0:4 * TK, 0:4 * TK], kvs[s, :, D + h * LANES:D + (h + 1) * LANES])
                 o = jnp.where(low, o2[:2 * TK], o2[2 * TK:]).astype(BF)
                 rows = pl.ds(pl.multiple_of(s * TK, TK), TK)
                 obuf[i, core, rows, cols] = o[:TK]
@@ -165,20 +192,26 @@
     def project(i, par, layer, step, n):
         o_copy(i).wait()
         ov = obuf[i].reshape(R, D)
-        for t in range(DT):
-            cols = slice(t * W, (t + 1) * W)
-            x[i, :, cols] = x[i, :, cols] + mm(ov, so[:, cols])
+        for r in range(0, R, R // 2):
+            for t in range(DT):
+                cols = slice(t * W, (t + 1) * W)
+                x[i, r:r + R // 2, cols] = x[i, r:r + R // 2, cols] + mm(ov[r:r + R // 2], so[:, cols])
         for a in range(CH):
-            ut[i, a * TK:(a + 1) * TK, :] = modulated(i, a, layer, step, 1)
+            def put(r, v, a=a):
+                ut[i, a * TK + r:a * TK + r + NR, :] = v
+
+            modulated(i, a, layer, step, 1, put)
 
         @pl.when((i == NC - 1) & (n >= 2))
         def _():
             pl.semaphore_wait(credit, 1)
 
         ut_copy(par, i).start()
+
+    def own_qkv(i, layer):
         uv = ut[i]
         for t in range(3 * DT):
-            y = mm(uv, tqkv[layer, :, t * W:(t + 1) * W])
+            y = mm_t(uv, tqkv[layer, t * W:(t + 1) * W, :])
             kind, tt = t // DT, t % DT
             if kind == 0:
                 y = y * qscale
@@ -195,7 +228,7 @@
         ut_copy(par, i).wait()
         uv = utr[par, i]
         for t in range(2 * DT):
-            y = mm(uv, tqkv[layer, :, D + t * W:D + (t + 1) * W])
+            y = mm_t(uv, tqkv[layer, D + t * W:D + (t + 1) * W, :])
             kind, tt = t // DT, t % DT
             ref = vt if kind else kt
             y4 = y.reshape(CH, G, SUB, W)
@@ -211,44 +244,50 @@
         for h in range(HP):
             bm[h] = jnp.where(valid, bias[layer, h], -jnp.inf)
 
-        @pl.loop(0, G // 2)
+        @pl.loop(0, G // TU)
         def _(gg):
             qrows = pl.ds(pl.multiple_of(i * CR, CR), CR)
             krows = pl.ds(pl.multiple_of(i * CR, CR), WIN)
-            units = [(gg * 2 + d, d * 2 * CR, h) for d in range(2) for h in range(HP)]
+            units = [(gg * TU + d, d * 2 * CR, h) for d in range(TU) for h in range(HP)]
             for g, r, h in units:
                 cols = slice(h * LANES, (h + 1) * LANES)
-                sc[h, r:r + 2 * CR, 0:WIN] = mm_t(stack_heads(qt[g, qrows, cols]), kt[g, krows, cols]) + bm[h]
-            for g, r, h in units:
-                pb[h, r:r + 2 * CR, 0:WIN] = softmax_rows(sc[h, r:r + 2 * CR, 0:WIN])
+                sv = mm_t(stack_heads(qt[g, qrows, cols]), kt[g, krows, cols]) + bm[h]
+                pb[h, r:r + 2 * CR, 0:WIN] = softmax_rows(sv)
             for g, r, h in units:
                 cols = slice(h * LANES, (h + 1) * LANES)
                 o2 = mm(pb[h, r:r + 2 * CR, 0:WIN], vt[g, krows, cols])
                 ob[pl.ds(pl.multiple_of(g * CR, CR), CR), cols] = jnp.where(low, o2[:CR], o2[CR:]).astype(BF)
 
         ov = ob[...]
-        for t in range(DT):
-            cols = slice(t * W, (t + 1) * W)
-            y4 = mm(ov, to[:, cols]).reshape(G, CH, SUB, W)
-            for a in range(CH):
-                x[i, a * TK:(a + 1) * TK, cols] = x[i, a * TK:(a + 1) * TK, cols] + y4[:, a].reshape(TK, W)
+        for r in range(0, R, R // 2):
+            for t in range(DT):
+                cols = slice(t * W, (t + 1) * W)
+                r0, r1 = r, r + R // 2
+                g0, gn = r0 // CR, (r1 - r0) // CR
+                y4 = mm(ov[r0:r1], to[:, cols]).reshape(gn, CH, SUB, W)
+                for a in range(CH):
+                    rows = slice(a * TK + g0 * SUB, a * TK + (g0 + gn) * SUB)
+                    x[i, rows, cols] = x[i, rows, cols] + y4[:, a].reshape(gn * SUB, W)
 
     def mlp(i, layer, step):
         for a in range(CH):
-            uu[a * TK:(a + 1) * TK, :] = modulated(i, a, layer, step, 2)
+            def put(r, v, a=a):
+                uu[a * TK + r:a * TK + r + NR, :] = v
+
+            modulated(i, a, layer, step, 2, put)
         uv = uu[...]
         for t in range(FF // FT):
             hp = mm(uv, up[:, t * FT:(t + 1) * FT])
-            for r in range(0, R, 128):
+            for r in range(0, R, min(R, 128)):
                 hb[r:r + 128, t * FT:(t + 1) * FT] = gelu(hp[r:r + 128]).astype(BF)
-        for t in range(DT):
-            cols = slice(t * W, (t + 1) * W)
-            for r in range(0, R, 256):
-                x[i, r:r + 256, cols] = x[i, r:r + 256, cols] + mm(hb[r:r + 256], down[:, cols])
+        for r in range(0, R, R // 2):
+            for t in range(DT):
+                cols = slice(t * W, (t + 1) * W)
+                x[i, r:r + R // 2, cols] = x[i, r:r + R // 2, cols] + mm(hb[r:r + R // 2], down[:, cols])
 
     def finish(i, step):
-        for a in range(CH):
-            uu[a * TK:(a + 1) * TK, :] = norm(x[i, a * TK:(a + 1) * TK, :]).astype(BF)
+        for r in range(0, R, NR):
+            uu[r:r + NR, :] = norm(x[i, r:r + NR, :]).astype(BF)
         v = mm(uu[...], w_out[...])
         for a in range(CH):
             row = i * CH + a + (S - 1) - step
@@ -267,7 +306,10 @@
 
     def launch(i, par, layer, step):
         for a in range(CH):
-            ust[i, a // HS, (a % HS) * TK:(a % HS + 1) * TK, :] = modulated(i, a, layer, step, 0)
+            def put(r, v, a=a):
+                ust[i, a // HS, (a % HS) * TK + r:(a % HS) * TK + r + NR, :] = v
+
+            modulated(i, a, layer, step, 0, put)
         for c in us_copies(par, i):
             c.start()
 
@@ -290,10 +332,19 @@
             for k in (2, 3, 4):
                 w_copy(k, layer).start()
 
-            @pl.loop(0, NC)
+            @pl.loop(0, NC + 1)
             def _(c):
-                spatial(NC - 1 - c, par)
-                project(NC - 1 - c, par, layer, step, n)
+                @pl.when(c < NC)
+                def _():
+                    spatial(NC - 1 - c, par)
+
+                @pl.when(c > 0)
+                def _():
+                    own_qkv(NC - c, layer)
+
+                @pl.when(c < NC)
+                def _():
+                    project(NC - 1 - c, par, layer, step, n)
 
             for k in (2, 3, 4):
                 w_copy(k, layer).wait()
@@ -338,6 +389,8 @@
     HP = D // LANES
     KR = (NC - 1) * CR + WIN
     scr = [
+        pltpu.VMEM((S - 1 + NC * CH, 6 * L + 1, D), F32),
+        pltpu.VMEM((L, HP, 2 * CR, WIN), F32),
         pltpu.VMEM((NC, R, D), F32),
         pltpu.VMEM((NC, 2, RH, D), BF),
         pltpu.VMEM((2, NC, 3, RH, D), BF),
@@ -350,15 +403,14 @@
         pltpu.VMEM((G, SR, D), BF),
         pltpu.VMEM((G, KR, D), BF),
         pltpu.VMEM((G, KR, D), BF),
-        pltpu.VMEM((HP, max(4 * TK, 4 * CR), max(4 * TK, WIN)), F32),
-        pltpu.VMEM((HP, max(4 * TK, 4 * CR), max(4 * TK, WIN)), BF),
+        pltpu.VMEM((max(2, 2) * HP, max(4 * TK, 8 * CR), max(4 * TK, WIN)), BF),
         pltpu.VMEM((HP, 2 * CR, WIN), F32),
         pltpu.VMEM((R, D), BF),
         pltpu.VMEM((R, D), BF),
         pltpu.VMEM((R, FF), BF),
-        pltpu.VMEM((D, 3 * D), BF),
+        pltpu.VMEM((3 * D, D), BF),
         pltpu.VMEM((D, D), BF),
-        pltpu.VMEM((L, D, 3 * D), BF),
+        pltpu.VMEM((L, 3 * D, D), BF),
         pltpu.VMEM((D, D), BF),
         pltpu.VMEM((D, FF), BF),
         pltpu.VMEM((FF, D), BF),
@@ -369,6 +421,7 @@
         pltpu.SemaphoreType.DMA((NC,)),
         pltpu.SemaphoreType.DMA((2, NC)),
         pltpu.SemaphoreType.DMA((5 + L,)),
+        pltpu.SemaphoreType.DMA((2,)),
         pltpu.SemaphoreType.REGULAR,
     ]
     inner = pl.BlockSpec(memory_space=pltpu.VMEM)
@@ -376,24 +429,12 @@
     return pl.pallas_call(
         functools.partial(kernel, cfg),
         out_shape=(jax.ShapeDtypeStruct((NC, R, LANES), F32), jax.ShapeDtypeStruct((S, TK, LANES), F32)),
-        in_specs=[inner] * 6 + [outer] * 6,
+        in_specs=[pl.BlockSpec(memory_space=pltpu.SMEM)] + [inner] * 4 + [outer] * 8,
         out_specs=(inner, inner),
         scratch_shapes=scr,
         compiler_params=pltpu.CompilerParams(collective_id=0, has_side_effects=True, vmem_limit_bytes=vmem),
         name="fifo_denoise",
     )(*args)
-
-
-def lag_bias_tiles(lag_bias, CH, SLOTS, WIN):
-    L, H, window = lag_bias.shape
-    a = jnp.arange(CH)[:, None, None, None]
-    tq = jnp.arange(SUB)[None, :, None, None]
-    k = jnp.arange(WIN // SUB)[None, None, :, None]
-    tk = jnp.arange(SUB)[None, None, None, :]
-    lag = SLOTS + a - k
-    ok = (lag >= 0) & (lag < window) & (tq == tk)
-    tiles = jnp.where(ok, jnp.take(lag_bias, jnp.clip(lag, 0, window - 1), axis=2), -jnp.inf)
-    return tiles.reshape(L, H // 2, 2 * CH * SUB, WIN)
 
 
 def solution(mesh):
@@ -406,6 +447,15 @@
     to_sib = [(f, f ^ 1) for f in range(MF)]
     to_next_chip = [(f, (f + 2) % MF) for f in range(MF)]
 
+    def seat(blk, q):
+        here = [t for t in range(MT) if (t // 2 + blk // 2) % 2 == blk % 2 and ((t + 1) // 2) % 2 == q // 2]
+        return here[0] * MF + 2 * (blk // 2) + q % 2
+
+    places = [(blk, q) for blk in range(MF) for q in range(MT)]
+    to_seat = [(q * MF + blk, seat(blk, q)) for blk, q in places]
+    to_home = [(seat(blk, q), q * MF + blk) for blk, q in places]
+    to_home_before = [(seat(blk, q), q * MF + (blk - 1) % MF) for blk, q in places]
+
     def body(z_loc, mod_loc, step_loc, noise_loc, lag_bias, w_in, w_out, w_sqkv, w_so, w_tqkv, w_to, w_up, w_down):
         SL, TK, C = z_loc.shape
         S = noise_loc.shape[0]
@@ -415,48 +465,37 @@
         CH = SL // NC
         WIN = 2 * SL * SUB
         tok, frm, chip, core, odd, half = roles(MT, MF)
-        quarter = 2 * half + core
-
+        both = ("tokens", "frames")
         zn = jnp.concatenate([z_loc.reshape(SL, TK * C), noise_loc.reshape(S, TK * C)], axis=0)
-        zn = lax.all_gather(zn, "tokens", axis=0)
-        zq = lax.dynamic_index_in_dim(zn, quarter, axis=0, keepdims=False)
-        sent = lax.dynamic_index_in_dim(zn, 2 * half + (1 - core), axis=0, keepdims=False)[:SL]
-        z_sib = lax.ppermute(sent, "frames", to_sib)
-        z_own = jnp.where(odd == core, zq[:SL], z_sib).reshape(SL, TK, C)
-        noise = zq[SL:].reshape(S, TK, C)
+        zn = lax.ppermute(zn, both, to_seat)
+        z_own = zn[:SL].reshape(SL, TK, C)
+        noise = zn[SL:].reshape(S, TK, C)
         pad = lambda v: jnp.pad(v, ((0, 0),) * (v.ndim - 1) + ((0, LANES - C),))
 
-        table = jnp.concatenate([mod_loc.reshape(SL, L * 6, D), jnp.broadcast_to(step_loc[:, None, None], (SL, 1, D))], axis=1)
+        table = jnp.concatenate([jnp.swapaxes(mod_loc, 1, 2).reshape(SL, 6 * L, D), jnp.broadcast_to(step_loc[:, None, None], (SL, 1, D))], axis=1)
         table_sib = lax.ppermute(table, "frames", to_sib)
         even_blk = jnp.where(core == 0, table, table_sib)
         odd_blk = jnp.where(core == 1, table, table_sib)
         tail = lax.ppermute(odd_blk[SL - (S - 1):], "frames", to_next_chip)
         own_tab = jnp.where(odd == 0, even_blk, odd_blk)
         prev_tab = jnp.where(odd == 0, tail, even_blk[SL - (S - 1):])
-        mod = jnp.concatenate([prev_tab, own_tab], axis=0)
-
+
+        by_output = lambda w: jnp.transpose(w, (0, 2, 3, 4, 1)).reshape(L, 3 * D, D)
         cfg = (L, S, NC, CH, TK, D, FF, HD, MT, MF, WIN)
         z_new, emit = denoise_call(
             cfg, 67043328,
-            pad(z_own).reshape(NC, CH * TK, LANES), mod, pad(noise), lag_bias_tiles(lag_bias, CH, SL, WIN),
-            jnp.pad(w_in, ((0, LANES - C), (0, 0))), jnp.pad(w_out, ((0, 0), (0, LANES - C))),
-            w_sqkv.reshape(L, D, 3 * D), w_so.reshape(L, D, D), w_tqkv.reshape(L, D, 3 * D), w_to.reshape(L, D, D), w_up, w_down,
+            lag_bias.reshape(L * lag_bias.shape[1], -1), pad(z_own).reshape(NC, CH * TK, LANES), pad(noise),
+            jnp.pad(w_in, ((0, LANES - C), (0, 0))), jnp.pad(w_out, ((0, 0), (0, LANES - C))), own_tab, prev_tab,
+            by_output(w_sqkv), w_so.reshape(L, D, D), by_output(w_tqkv), w_to.reshape(L, D, D), w_up, w_down,
         )
 
         mine = jnp.concatenate([z_new.reshape(SL, TK, LANES)[:, :, :C].reshape(SL, TK * C), emit[:, :, :C].reshape(S, TK * C)], axis=0)
-        every = lax.all_gather(mine, ("tokens", "frames"), axis=0)
-        where_is = []
-        for blk in range(MF):
-            for q in range(MT):
-                xx, o, hf, cc = blk // 2, blk % 2, q // 2, q % 2
-                ty = [t for t in range(MT) if (t // 2 + xx) % 2 == o and ((t + 1) // 2) % 2 == hf]
-                where_is.append(ty[0] * MF + 2 * xx + cc)
-        queue = jnp.stack([every[d, :SL] for d in where_is]).reshape(MF, MT, SL, TK * C)
-        queue = jnp.roll(jnp.swapaxes(queue, 1, 2).reshape(MF * SL, MT, TK * C), -S, axis=0)
-        z_fin = lax.dynamic_slice(queue, (frm * SL, tok, 0), (SL, 1, TK * C)).reshape(SL, TK, C)
-        em = jnp.stack([every[where_is[q], SL:] for q in range(MT)])
+        late = lax.ppermute(mine[S:], both, to_home)
+        early = lax.ppermute(mine[:S], both, to_home_before)
+        z_fin = jnp.concatenate([late[:SL - S], early], axis=0).reshape(SL, TK, C)
         per = TK // MF
-        em = lax.dynamic_slice(em, (tok, 0, frm * per * C), (1, S, per * C)).reshape(S, per, C)
+        em = jnp.swapaxes(late[SL - S:].reshape(S, MF, per * C), 0, 1)
+        em = lax.all_to_all(em, "frames", 0, 0, tiled=True)[0].reshape(S, per, C)
         return em, z_fin
 
     return jax.shard_map(body, mesh=mesh, in_specs=(slot_spec, mod_spec, step_spec, noise_spec) + (P(),) * 9, out_specs=(emit_spec, slot_spec), check_vma=False)

time: 878 us -> 665 us (0.76)
  Pallas kernels: 739 us -> 621 us
  local copies, waits for them, and re-layouts: 76.9 us -> 14.5 us
  blocking collectives: 37.9 us -> 0 us
  starting transfers between devices: 6.21 us -> 20.8 us
    pallas_call x1, Pallas kernels: 739 us -> 621 us  [denoise_call(): pl.pallas_call(functools.partial(kernel, cfg), out_shape=(jax.ShapeDtypeS...]
    broadcast_in_dim x4 -> x0, local copies, waits for them, and re-layouts: 41.2 us -> none  [lag_bias_tiles(): jnp.where(ok, jnp.take(lag_bias, jnp.clip(lag, 0, window - 1), axis=2), -...]
    all_gather x2 -> x0, blocking collectives: 37.9 us -> none  [the longest x1 27.7 us: body(): every = lax.all_gather(mine, ('tokens', 'frames'), axis=0)]
    reshape x5 -> x6, local copies, waits for them, and re-layouts: 21.7 us -> 1.23 us  [the longest x2 0.61 us: body(): lag_bias.reshape(L * lag_bias.shape[1], -1)]
    ppermute x1 -> x3, starting transfers between devices: 2.75 us -> 14.3 us  [the longest x1 7.03 us: body(): zn = lax.ppermute(zn, both, to_seat)]
  transfers between devices with their start and end apart: 3 -> 6, of which waited for: 1 -> 2; matrix products, arithmetic and copies ran while one was open for 8% -> 1% of each run, Pallas kernels for 0% -> 0%
where the time goes in v2:
time: 665 us
  Pallas kernels  621 us (93%)
  starting transfers between devices  20.8 us (3%)
  local copies, waits for them, and re-layouts  14.5 us (2%)
    pallas_call x1, Pallas kernels, denoise_call(): pl.pallas_call(functools.partial(kernel, cfg), out_shape=(jax.ShapeDtypeS...  621 us
  transfers between devices with their start and end apart: 6, of which 2 were waited for; matrix products, arithmetic and copies ran while one was open for 1% of the time, Pallas kernels for 0%

profile of v2, /device:TPU:97, one launch (start us, length us, event | category | flops | bytes accessed | tf_op | source)
XLA Modules:
  0.0 665.0 jit_solution(3557100714514081738)
XLA Ops:
  0.7 1.2 copy.40
  1.9 0.4 copy.41
  2.3 0.7 broadcast_in_dim.2
  3.0 0.1 pad_maximum_fusion
  3.1 0.4 copy.42
  3.5 2.1 collective-permute-start.1
  5.6 1.7 collective-permute-done.1
  7.3 1.4 broadcast_select_fusion
  8.7 0.8 collective-permute-start.2
  9.5 0.0 copy-done.1
  9.5 0.1 copy.35
  9.7 0.1 reshape.58
  9.8 0.1 copy.34
  10.0 0.1 copy.36
  10.0 7.0 %collective-permute-start = (f32[22,256]{1,0:T(8,128)S(1)}, f32[22,256]{1,0:T(8,128)S(1)}, u32[]{:S(2)}, u32[]{:S(2)}) collective-permute-start(f32[22,256]{1,0:T(8,128)S(1)} %pad_maximum_fusion.1), channel_id=1, source_target_pairs={{0,0},{8,1},{16,8},{24,9},{1,24},{9,25},{17,16},{25,17},{2,26},{10... | collective-permute-start | bytes 67592 | tf_op jit(solution)/shard_map/ppermute | solution.py:470
  17.1 0.2 copy.39
  17.2 0.7 pad.19.w_out
  18.0 0.7 pad.18.w_in
  18.7 0.6 reshape.72.lag_bias
  19.3 0.0 collective-permute-done
  19.3 0.1 copy.37
  19.4 0.6 copy.54
  20.0 0.2 reshape.61
  20.2 0.9 pad.16.clone
  21.1 0.7 pad.17.noise
  21.8 0.0 collective-permute-done.2
  21.8 0.7 slice_select_fusion.prev_tab
  22.5 620.7 %fifo_denoise.1 = (f32[4,256,128]{2,1,0:T(8,128)}, f32[6,64,128]{2,1,0:T(8,128)}) custom-call(f32[24,16]{1,0:T(8,128)} %reshape.72.lag_bias, f32[4,256,128]{2,1,0:T(8,128)} %bitcast.28, f32[6,64,128]{2,1,0:T(8,128)} %pad.17.noise, bf16[128,768]{1,0:T(8,128)(2,1)} %pad.18.w_in, bf16[768,128]{1,0:T(8,128)(2,1)} %pad.19.w_out, ...), custom_call_target="tpu_custom_call" | custom-call | tf_op jit(solution)/shard_map/fifo_denoise/pallas_call | solution.py:429
  643.2 1.5 copy.46
  644.7 0.1 copy.47
  644.8 1.1 reshape.69
  645.9 2.7 collective-permute-start.3
  648.5 0.9 slice.57
  649.5 0.1 slice.48
  649.6 4.6 collective-permute-start.4
  654.2 0.0 collective-permute-done.3
  654.2 0.1 reshape.70
  654.3 0.7 reshape.73
  655.0 3.5 all-to-all-start
  658.5 0.0 collective-permute-done.4
  658.6 0.1 copy.49
  658.7 0.7 copy.51
  659.4 3.6 all-to-all-done
  663.0 0.5 broadcast.14
  663.5 0.7 reduce
  664.2 0.1 reshape.74
  664.2 0.1 reshape_squeeze.3
  664.3 0.7 copy.50
  (19 shorter events, 0.1 us)
Async XLA Ops:
  0.6 8.9 %copy-start.1 = (f32[6,64,4]{1,2,0:T(4,128)S(1)}, f32[6,64,4]{1,2,0:T(4,128)}, u32[]{:S(2)}) copy-start(f32[6,64,4]{1,2,0:T(4,128)} %param.16) | copy-start | bytes 18436
  0.6 9.2 %copy-start = (f32[16,64,4]{1,2,0:T(4,128)S(1)}, f32[16,64,4]{1,2,0:T(4,128)}, u32[]{:S(2)}) copy-start(f32[16,64,4]{1,2,0:T(4,128)} %param.13) | copy-start | bytes 49156
  0.7 16.4 %copy-start.3 = (bf16[768,4]{0,1:T(4,128)(2,1)S(1)}, bf16[768,4]{0,1:T(4,128)(2,1)}, u32[]{:S(2)}) copy-start(bf16[768,4]{0,1:T(4,128)(2,1)} %param.19) | copy-start | bytes 18436
  0.7 17.3 %copy-start.4 = (bf16[4,768]{1,0:T(4,128)(2,1)S(1)}, bf16[4,768]{1,0:T(4,128)(2,1)}, u32[]{:S(2)}) copy-start(bf16[4,768]{1,0:T(4,128)(2,1)} %param.18) | copy-start | bytes 18436
  0.7 18.0 %copy-start.2 = (f32[2,12,16]{2,0,1:T(2,128)S(1)}, f32[2,12,16]{2,0,1:T(2,128)}, u32[]{:S(2)}) copy-start(f32[2,12,16]{2,0,1:T(2,128)} %param.17) | copy-start | bytes 4612
  3.5 3.8 collective-permute-start.1
  8.7 13.1 %collective-permute-start.2 = (f32[5,13,768]{2,1,0:T(8,128)S(1)}, f32[5,13,768]{2,1,0:T(8,128)S(1)}, u32[]{:S(2)}, u32[]{:S(2)}) collective-permute-start(f32[5,13,768]{2,1,0:T(8,128)S(1)} %slice.51), channel_id=1, source_target_pairs={{0,2},{1,3},{2,4},{3,5},{4,6},{5,7},{6,0},{7,1},{8,10},{9,11},{10,... | collective-permute-start | bytes 599048 | tf_op jit(solution)/shard_map/ppermute | solution.py:479
  10.0 9.3 %collective-permute-start = (f32[22,256]{1,0:T(8,128)S(1)}, f32[22,256]{1,0:T(8,128)S(1)}, u32[]{:S(2)}, u32[]{:S(2)}) collective-permute-start(f32[22,256]{1,0:T(8,128)S(1)} %pad_maximum_fusion.1), channel_id=1, source_target_pairs={{0,0},{8,1},{16,8},{24,9},{1,24},{9,25},{17,16},{25,17},{2,26},{10... | collective-permute-start | bytes 67592 | tf_op jit(solution)/shard_map/ppermute | solution.py:470
  645.9 8.4 %collective-permute-start.3 = (f32[16,256]{1,0:T(8,128)S(1)}, f32[16,256]{1,0:T(8,128)S(1)}, u32[]{:S(2)}, u32[]{:S(2)}) collective-permute-start(f32[16,256]{1,0:T(8,128)S(1)} %pad_maximum_fusion.2), channel_id=1, source_target_pairs={{0,0},{1,8},{8,16},{9,24},{24,1},{25,9},{16,17},{17,25},{26,2},{27... | collective-permute-start | bytes 49160 | tf_op jit(solution)/shard_map/ppermute | solution.py:493
  649.6 8.9 %collective-permute-start.4 = (f32[6,256]{1,0:T(8,128)S(1)}, f32[6,256]{1,0:T(8,128)S(1)}, u32[]{:S(2)}, u32[]{:S(2)}) collective-permute-start(f32[6,256]{1,0:T(8,128)S(1)} %slice.48), channel_id=1, source_target_pairs={{0,7},{1,15},{8,23},{9,31},{24,0},{25,8},{16,16},{17,24},{26,1},{2... | collective-permute-start | bytes 18440 | tf_op jit(solution)/shard_map/ppermute | solution.py:494
  655.0 8.0 %all-to-all-start = ((f32[8,1,192]{2,1,0:T(1,128)}), f32[8,1,192]{2,1,0:T(1,128)S(1)}, u32[]{:S(2)}, u32[]{:S(2)}) async-start(f32[8,1,192]{2,1,0:T(1,128)} %reshape.73), calls=%async_computation | async-start | bytes 16384 | tf_op jit(solution)/shard_map/all_to_all | solution.py:498

commit v3 on v2

--- a/solution.py
+++ b/solution.py
@@ -43,7 +43,7 @@
     return tok, frm, chip, core, odd, half
 
 
-def kernel(cfg, lag_bias, z_in, noise, w_in, w_out, own_tab, prev_tab, sqkv_h, so_h, tqkv_h, to_h, up_h, down_h, z, emit,
+def kernel(cfg, lag_bias, z_in, z_near, noise, w_in, w_out, own_tab, prev_tab, sqkv_h, so_h, tqkv_h, to_h, up_h, down_h, z, emit,
            mod, bias, x, ust, us, kvs, qs, obuf, osnd, ut, utr, qt, kt, vt, pb, bm, ob, uu, hb,
            sqkv, so, tqkv, to, up, down,
            us_s, us_r, o_s, o_r, ut_s, ut_r, w_sem, t_sem, credit):
@@ -57,7 +57,7 @@
     DT = D // W
     FT = min(256, FF)
     qscale = HD ** -0.5
-    SU, TU, RS = min(2, HS), min(4, G), min(64, 4 * TK)
+    SU, TU, RS = min(2, HS), min(8, G), min(64, 4 * TK)
 
     vid = lax.axis_index("videos")
     tok, frm, chip, core, odd, _ = roles(MT, MF)
@@ -107,11 +107,19 @@
     def o_copy(i):
         return remote(osnd.at[i], obuf.at[i, core], o_s.at[i], o_r.at[i], sib)
 
-    def ut_copy(par, i):
-        return remote(ut.at[i], utr.at[par, i], ut_s.at[i], ut_r.at[par, i], nxt)
+    unread = TK * max(0, min(NC * CH + 1 - lag_bias.shape[1], CH - 1))
+
+    def ut_each(par, i, act):
+        def part(row):
+            act(remote(ut.at[i, row:R], utr.at[par, i, row:R], ut_s.at[i], ut_r.at[par, i], nxt))
+
+        pl.when(i == 0)(lambda: part(unread))
+        pl.when(i > 0)(lambda: part(0))
 
     z[...] = z_in[...]
     emit[...] = jnp.zeros_like(emit)
+    if unread:
+        utr[:, 0, 0:unread, :] = jnp.zeros((2, unread, D), BF)
     for g in range(G):
         for ref in (kt, vt):
             ref[g] = jnp.zeros(ref.shape[1:], BF)
@@ -146,17 +154,22 @@
 
     NR = min(32, TK)
 
+    def affine(slot, layer, step, which):
+        row = slot + (S - 1) - step
+        return 1.0 + mod[row, pl.ds((2 * which + 1) * L + layer, 1), :], mod[row, pl.ds(2 * which * L + layer, 1), :]
+
     def modulated(i, a, layer, step, which, put):
-        row = i * CH + a + (S - 1) - step
-        shift = mod[row, pl.ds(2 * which * L + layer, 1), :]
-        gain = 1.0 + mod[row, pl.ds((2 * which + 1) * L + layer, 1), :]
+        gain, shift = affine(i * CH + a, layer, step, which)
         for r in range(0, TK, NR):
             xv = x[i, a * TK + r:a * TK + r + NR, :]
             put(r, (norm(xv) * gain + shift).astype(BF))
 
-    def spatial(i, par):
-        for c in us_copies(par, i):
-            c.wait()
+    def spatial(i, par, n):
+        @pl.when(n > 0)
+        def _():
+            for c in us_copies(par, i):
+                c.wait()
+
         own = ust[i, core]
         u_all = jnp.concatenate([own, us[par, i, 0], us[par, i, 1], us[par, i, 2]], axis=0)
         u_q = jnp.concatenate([own, us[par, i, 0]], axis=0)
@@ -206,7 +219,7 @@
         def _():
             pl.semaphore_wait(credit, 1)
 
-        ut_copy(par, i).start()
+        ut_each(par, i, lambda c: c.start())
 
     def own_qkv(i, layer):
         uv = ut[i]
@@ -225,7 +238,7 @@
                     ref[g, pl.ds(pl.multiple_of(SR + i * CR, CR), CR), tt * W:(tt + 1) * W] = yg
 
     def temporal(i, par, layer, step):
-        ut_copy(par, i).wait()
+        ut_each(par, i, lambda c: c.wait())
         uv = utr[par, i]
         for t in range(2 * DT):
             y = mm_t(uv, tqkv[layer, D + t * W:D + (t + 1) * W, :])
@@ -285,33 +298,44 @@
                 cols = slice(t * W, (t + 1) * W)
                 x[i, r:r + R // 2, cols] = x[i, r:r + R // 2, cols] + mm(hb[r:r + R // 2], down[:, cols])
 
-    def finish(i, step):
-        for r in range(0, R, NR):
-            uu[r:r + NR, :] = norm(x[i, r:r + NR, :]).astype(BF)
-        v = mm(uu[...], w_out[...])
-        for a in range(CH):
-            row = i * CH + a + (S - 1) - step
-            dt = mod[row, pl.ds(6 * L, 1), 0:LANES]
-            z[i, a * TK:(a + 1) * TK, :] = z[i, a * TK:(a + 1) * TK, :] + dt * v[a * TK:(a + 1) * TK]
-
-        @pl.when(i == step // CH)
-        def _():
-            rows = pl.ds(pl.multiple_of((step % CH) * TK, TK), TK)
-            zv = z[i, rows, :]
-            emit[step] = zv
-            z[i, rows, :] = jnp.where(first, noise[step], zv)
-
-    def enter(i):
-        x[i] = mm(z[i].astype(BF), w_in[...]).astype(BF).astype(F32)
-
-    def launch(i, par, layer, step):
+    def embed(zv):
+        return mm(zv.astype(BF), w_in[...]).astype(BF).astype(F32)
+
+    def ready(i, layer, step):
         for a in range(CH):
             def put(r, v, a=a):
                 ust[i, a // HS, (a % HS) * TK + r:(a % HS) * TK + r + NR, :] = v
 
             modulated(i, a, layer, step, 0, put)
-        for c in us_copies(par, i):
-            c.start()
+
+    def turn(i, step):
+        for r in range(0, R, RH):
+            for q in range(r, r + RH, NR):
+                uu[q:q + NR, :] = norm(x[i, q:q + NR, :]).astype(BF)
+            v = mm(uu[r:r + RH], w_out[...])
+            entering = []
+            for a in range(r // TK, (r + RH) // TK):
+                dt = mod[i * CH + a + (S - 1) - step, pl.ds(6 * L, 1), 0:LANES]
+                zv = z[i, a * TK:(a + 1) * TK, :] + dt * v[a * TK - r:(a + 1) * TK - r]
+                z[i, a * TK:(a + 1) * TK, :] = zv
+                entering.append(jnp.where(first & (i * CH + a == step), noise[step], zv))
+            x[i, r:r + RH, :] = embed(jnp.concatenate(entering, axis=0))
+
+    def replace_head(step):
+        rows = pl.ds(pl.multiple_of((step % CH) * TK, TK), TK)
+        zv = z[step // CH, rows, :]
+        emit[step] = zv
+        z[step // CH, rows, :] = jnp.where(first, noise[step], zv)
+
+    def begin(i):
+        x[i] = embed(z[i])
+        ready(i, 0, 0)
+        mine = pl.ds(pl.multiple_of(core * RH, RH), RH)
+        for k in range(3):
+            xv = embed(z_near[k, i, mine, :])
+            for s in range(HS):
+                gain, shift = affine(i * CH + core * HS + s, 0, 0, 0)
+                us[0, i, k, s * TK:(s + 1) * TK, :] = (norm(xv[s * TK:(s + 1) * TK]) * gain + shift).astype(BF)
 
     @pl.loop(0, NT + 1)
     def _(m):
@@ -336,7 +360,7 @@
             def _(c):
                 @pl.when(c < NC)
                 def _():
-                    spatial(NC - 1 - c, par)
+                    spatial(NC - 1 - c, par, n)
 
                 @pl.when(c > 0)
                 def _():
@@ -358,22 +382,29 @@
         def _(c):
             i = NC - 1 - c
 
+            @pl.when(m == 0)
+            def _():
+                begin(i)
+
             @pl.when(m > 0)
             def _():
                 temporal(i, par, layer, step)
                 mlp(i, layer, step)
+                ready(i, nlayer, jnp.minimum(nstep, S - 1))
 
                 @pl.when(layer == L - 1)
                 def _():
-                    finish(i, step)
-
-            @pl.when(m < NT)
-            def _():
-                @pl.when(nlayer == 0)
+                    turn(i, step)
+                    ready(i, nlayer, jnp.minimum(nstep, S - 1))
+
+                @pl.when(m < NT)
                 def _():
-                    enter(i)
-
-                launch(i, npar, nlayer, nstep)
+                    for c in us_copies(npar, i):
+                        c.start()
+
+        @pl.when((m > 0) & (layer == L - 1))
+        def _():
+            replace_head(step)
 
         @pl.when(m > 0)
         def _():
@@ -403,7 +434,7 @@
         pltpu.VMEM((G, SR, D), BF),
         pltpu.VMEM((G, KR, D), BF),
         pltpu.VMEM((G, KR, D), BF),
-        pltpu.VMEM((max(2, 2) * HP, max(4 * TK, 8 * CR), max(4 * TK, WIN)), BF),
+        pltpu.VMEM((max(2, 2) * HP, max(4 * TK, 16 * CR), max(4 * TK, WIN)), BF),
         pltpu.VMEM((HP, 2 * CR, WIN), F32),
         pltpu.VMEM((R, D), BF),
         pltpu.VMEM((R, D), BF),
@@ -429,7 +460,7 @@
     return pl.pallas_call(
         functools.partial(kernel, cfg),
         out_shape=(jax.ShapeDtypeStruct((NC, R, LANES), F32), jax.ShapeDtypeStruct((S, TK, LANES), F32)),
-        in_specs=[pl.BlockSpec(memory_space=pltpu.SMEM)] + [inner] * 4 + [outer] * 8,
+        in_specs=[pl.BlockSpec(memory_space=pltpu.SMEM)] + [inner] * 5 + [outer] * 8,
         out_specs=(inner, inner),
         scratch_shapes=scr,
         compiler_params=pltpu.CompilerParams(collective_id=0, has_side_effects=True, vmem_limit_bytes=vmem),
@@ -453,6 +484,7 @@
 
     places = [(blk, q) for blk in range(MF) for q in range(MT)]
     to_seat = [(q * MF + blk, seat(blk, q)) for blk, q in places]
+    to_near = [[((q ^ k) * MF + blk, seat(blk, q)) for blk, q in places] for k in (1, 2, 3)]
     to_home = [(seat(blk, q), q * MF + blk) for blk, q in places]
     to_home_before = [(seat(blk, q), q * MF + (blk - 1) % MF) for blk, q in places]
 
@@ -468,7 +500,7 @@
         both = ("tokens", "frames")
         zn = jnp.concatenate([z_loc.reshape(SL, TK * C), noise_loc.reshape(S, TK * C)], axis=0)
         zn = lax.ppermute(zn, both, to_seat)
-        z_own = zn[:SL].reshape(SL, TK, C)
+        z_all = jnp.concatenate([zn[:SL]] + [lax.ppermute(z_loc.reshape(SL, TK * C), both, p) for p in to_near], axis=0).reshape(4, SL, TK, C)
         noise = zn[SL:].reshape(S, TK, C)
         pad = lambda v: jnp.pad(v, ((0, 0),) * (v.ndim - 1) + ((0, LANES - C),))
 
@@ -481,10 +513,11 @@
         prev_tab = jnp.where(odd == 0, tail, even_blk[SL - (S - 1):])
 
         by_output = lambda w: jnp.transpose(w, (0, 2, 3, 4, 1)).reshape(L, 3 * D, D)
+        z_tiles = pad(z_all).reshape(4, NC, CH * TK, LANES)
         cfg = (L, S, NC, CH, TK, D, FF, HD, MT, MF, WIN)
         z_new, emit = denoise_call(
             cfg, 67043328,
-            lag_bias.reshape(L * lag_bias.shape[1], -1), pad(z_own).reshape(NC, CH * TK, LANES), pad(noise),
+            lag_bias.reshape(L * lag_bias.shape[1], -1), z_tiles[0], z_tiles[1:], pad(noise),
             jnp.pad(w_in, ((0, LANES - C), (0, 0))), jnp.pad(w_out, ((0, 0), (0, LANES - C))), own_tab, prev_tab,
             by_output(w_sqkv), w_so.reshape(L, D, D), by_output(w_tqkv), w_to.reshape(L, D, D), w_up, w_down,
         )

time: 665 us -> 675 us (1.015)
  local copies, waits for them, and re-layouts: 14.5 us -> 45.6 us
  Pallas kernels: 621 us -> 594 us
    slice x2 -> x4, local copies, waits for them, and re-layouts: 0.1 us -> 28.6 us  [the longest x2 16.3 us: body(): z_tiles[1:]]
    pallas_call x1, Pallas kernels: 621 us -> 594 us  [denoise_call(): pl.pallas_call(functools.partial(kernel, cfg), out_shape=(jax.ShapeDtypeS...]
    ppermute x0 -> x3, starting transfers between devices: none -> 11.2 us  [body(): lax.ppermute(z_loc.reshape(SL, TK * C), both, p)]
  transfers between devices with their start and end apart: 6 -> 9, of which waited for: 2 -> 1; matrix products, arithmetic and copies ran while one was open for 1% -> 6% of each run, Pallas kernels for 0% -> 0%
where the time goes in v3:
time: 675 us; the launch traced here: 674 us
  Pallas kernels  594 us (88%)
  local copies, waits for them, and re-layouts  45.6 us (7%)
  starting transfers between devices  26.9 us (4%)
    pallas_call x1, Pallas kernels, denoise_call(): pl.pallas_call(functools.partial(kernel, cfg), out_shape=(jax.ShapeDtypeS...  594 us
    slice x2, local copies, waits for them, and re-layouts, body(): z_tiles[1:]  16.3 us
  transfers between devices with their start and end apart: 9, of which 1 were waited for; matrix products, arithmetic and copies ran while one was open for 6% of the time, Pallas kernels for 0%

profile of v3, /device:TPU:97, one launch (start us, length us, event | category | flops | bytes accessed | tf_op | source)
XLA Modules:
  0.0 673.9 jit_solution(18293379127132855173)
XLA Ops:
  0.6 0.9 copy.56
  1.5 6.8 %collective-permute-start.3 = (f32[16,256]{0,1:T(8,128)S(1)}, f32[16,256]{0,1:T(8,128)S(1)}, u32[]{:S(2)}, u32[]{:S(2)}) collective-permute-start(f32[16,256]{0,1:T(8,128)S(1)} %bitcast.37), channel_id=1, source_target_pairs={{24,0},{16,1},{8,8},{0,9},{25,24},{17,25},{9,16},{1,17},{26,26},{1... | collective-permute-start | bytes 49160 | tf_op jit(solution)/shard_map/ppermute | solution.py:503
  8.3 2.4 collective-permute-start.2
  10.7 2.0 collective-permute-start.1
  12.7 0.8 copy.76
  13.5 0.1 pad_maximum_fusion.1
  13.6 4.7 collective-permute-start
  18.3 1.2 copy.63
  19.5 0.4 copy.64
  19.8 0.7 broadcast_in_dim.2
  20.6 0.1 pad_maximum_fusion
  20.7 0.4 copy.65
  21.1 0.1 collective-permute-start.4
  21.2 0.7 copy.75
  22.0 0.6 reshape.75.lag_bias
  22.6 0.9 copy.62
  23.4 1.4 pad.18.w_in
  24.8 0.7 pad.19.w_out
  25.6 0.2 pad_maximum_fusion.2
  25.8 0.3 reshape.63
  26.0 6.1 pad_slice_fusion
  32.1 1.4 broadcast_select_fusion
  33.5 0.9 collective-permute-start.5
  34.4 6.0 pad_slice_fusion.1
  40.4 6.3 copy.59
  46.7 10.2 %copy.60 = f32[3,16,64,128]{3,2,1,0:T(8,128)} copy(f32[3,16,64,128]{1,0,3,2:T(4,128)} %pad_slice_fusion) | data formatting | bytes 3145728 | tf_op jit(solution)/shard_map/slice | solution.py:520
  56.9 0.1 slice.63
  57.0 0.6 copy.77
  57.6 0.7 pad.17.noise
  58.3 0.7 slice_select_fusion.prev_tab
  59.0 593.9 %fifo_denoise.1 = (f32[4,256,128]{2,1,0:T(8,128)}, f32[6,64,128]{2,1,0:T(8,128)}) custom-call(f32[24,16]{1,0:T(8,128)} %reshape.75.lag_bias, f32[4,256,128]{2,1,0:T(8,128)} %bitcast.34, f32[3,4,256,128]{3,2,1,0:T(8,128)} %bitcast.30, f32[6,64,128]{2,1,0:T(8,128)} %pad.17.noise, bf16[128,768]{1,0:T(8,128)(2,1)} %pad.18.w_in, bf16[768,128]{1,0:T(8,128)(2,1)} %pad.19.w_out, ...), custom_call_target="tpu_custom_call" | custom-call | tf_op jit(solution)/shard_map/fifo_denoise/pallas_call | solution.py:460
  652.9 1.1 reshape.72
  654.0 1.5 copy.69
  655.5 2.2 collective-permute-start.6
  657.8 0.9 slice.70
  658.7 0.1 slice.61
  658.9 4.4 collective-permute-start.7
  663.3 0.1 reshape.73
  663.3 0.7 reshape.76
  664.0 3.5 all-to-all-start
  667.5 0.1 copy.72
  667.6 0.7 copy.74
  668.3 3.6 all-to-all-done
  671.9 0.5 broadcast.14
  672.4 0.7 reduce
  673.1 0.1 reshape.77
  673.2 0.1 reshape_squeeze.3
  673.2 0.7 copy.73
  (15 shorter events, 0.1 us)
Async XLA Ops:
  1.5 24.1 %collective-permute-start.3 = (f32[16,256]{0,1:T(8,128)S(1)}, f32[16,256]{0,1:T(8,128)S(1)}, u32[]{:S(2)}, u32[]{:S(2)}) collective-permute-start(f32[16,256]{0,1:T(8,128)S(1)} %bitcast.37), channel_id=1, source_target_pairs={{24,0},{16,1},{8,8},{0,9},{25,24},{17,25},{9,16},{1,17},{26,26},{1... | collective-permute-start | bytes 49160 | tf_op jit(solution)/shard_map/ppermute | solution.py:503
  8.3 17.3 %collective-permute-start.2 = (f32[16,256]{0,1:T(8,128)S(1)}, f32[16,256]{0,1:T(8,128)S(1)}, u32[]{:S(2)}, u32[]{:S(2)}) collective-permute-start(f32[16,256]{0,1:T(8,128)S(1)} %bitcast.38), channel_id=1, source_target_pairs={{16,0},{24,1},{0,8},{8,9},{17,24},{25,25},{1,16},{9,17},{18,26},{2... | collective-permute-start | bytes 49160 | tf_op jit(solution)/shard_map/ppermute | solution.py:503
  10.7 14.8 %collective-permute-start.1 = (f32[16,256]{0,1:T(8,128)S(1)}, f32[16,256]{0,1:T(8,128)S(1)}, u32[]{:S(2)}, u32[]{:S(2)}) collective-permute-start(f32[16,256]{0,1:T(8,128)S(1)} %bitcast.39), channel_id=1, source_target_pairs={{8,0},{0,1},{24,8},{16,9},{9,24},{1,25},{25,16},{17,17},{10,26},{2... | collective-permute-start | bytes 49160 | tf_op jit(solution)/shard_map/ppermute | solution.py:503
  13.6 11.9 %collective-permute-start = (f32[22,256]{0,1:T(8,128)S(1)}, f32[22,256]{0,1:T(8,128)S(1)}, u32[]{:S(2)}, u32[]{:S(2)}) collective-permute-start(f32[22,256]{0,1:T(8,128)S(1)} %pad_maximum_fusion.1), channel_id=1, source_target_pairs={{0,0},{8,1},{16,8},{24,9},{1,24},{9,25},{17,16},{25,17},{2,26},{10... | collective-permute-start | bytes 67592 | tf_op jit(solution)/shard_map/ppermute | solution.py:502
  21.1 11.1 %collective-permute-start.4 = (f32[16,13,768]{2,0,1:T(8,128)S(1)}, f32[16,13,768]{2,0,1:T(8,128)S(1)}, u32[]{:S(2)}, u32[]{:S(2)}) collective-permute-start(f32[16,13,768]{2,0,1:T(8,128)S(1)} %copy.65), channel_id=1, source_target_pairs={{0,1},{1,0},{2,3},{3,2},{4,5},{5,4},{6,7},{7,6},{8,9},{9,8},{10,11... | collective-permute-start | bytes 1916936 | tf_op jit(solution)/shard_map/ppermute | solution.py:508
  33.5 24.8 %collective-permute-start.5 = (f32[5,13,768]{2,1,0:T(8,128)S(1)}, f32[5,13,768]{2,1,0:T(8,128)S(1)}, u32[]{:S(2)}, u32[]{:S(2)}) collective-permute-start(f32[5,13,768]{2,1,0:T(8,128)S(1)} %slice.64), channel_id=1, source_target_pairs={{0,2},{1,3},{2,4},{3,5},{4,6},{5,7},{6,0},{7,1},{8,10},{9,11},{10,... | collective-permute-start | bytes 599048 | tf_op jit(solution)/shard_map/ppermute | solution.py:511
  655.5 7.7 %collective-permute-start.6 = (f32[16,256]{1,0:T(8,128)S(1)}, f32[16,256]{1,0:T(8,128)S(1)}, u32[]{:S(2)}, u32[]{:S(2)}) collective-permute-start(f32[16,256]{1,0:T(8,128)S(1)} %pad_maximum_fusion.3), channel_id=1, source_target_pairs={{0,0},{1,8},{8,16},{9,24},{24,1},{25,9},{16,17},{17,25},{26,2},{27... | collective-permute-start | bytes 49160 | tf_op jit(solution)/shard_map/ppermute | solution.py:526
  658.9 8.6 %collective-permute-start.7 = (f32[6,256]{1,0:T(8,128)S(1)}, f32[6,256]{1,0:T(8,128)S(1)}, u32[]{:S(2)}, u32[]{:S(2)}) collective-permute-start(f32[6,256]{1,0:T(8,128)S(1)} %slice.61), channel_id=1, source_target_pairs={{0,7},{1,15},{8,23},{9,31},{24,0},{25,8},{16,16},{17,24},{26,1},{2... | collective-permute-start | bytes 18440 | tf_op jit(solution)/shard_map/ppermute | solution.py:527
  664.0 7.9 %all-to-all-start = ((f32[8,1,192]{2,1,0:T(1,128)}), f32[8,1,192]{2,1,0:T(1,128)S(1)}, u32[]{:S(2)}, u32[]{:S(2)}) async-start(f32[8,1,192]{2,1,0:T(1,128)} %reshape.76), calls=%async_computation | async-start | bytes 16384 | tf_op jit(solution)/shard_map/all_to_all | solution.py:531

commit v4 on v3

--- a/solution.py
+++ b/solution.py
@@ -11,6 +11,7 @@
 BF = jnp.bfloat16
 F32 = jnp.float32
 LANES = 128
+CPAD = 16
 SUB = 8
 CHUNKS = 4
 
@@ -21,6 +22,10 @@
 
 def mm_t(a, b):
     return lax.dot_general(a, b, (((1,), (1,)), ((), ())), preferred_element_type=F32)
+
+
+def tt_mm(a, b):
+    return lax.dot_general(a, b, (((0,), (0,)), ((), ())), preferred_element_type=F32)
 
 
 def norm(xv):
@@ -43,10 +48,10 @@
     return tok, frm, chip, core, odd, half
 
 
-def kernel(cfg, lag_bias, z_in, z_near, noise, w_in, w_out, own_tab, prev_tab, sqkv_h, so_h, tqkv_h, to_h, up_h, down_h, z, emit,
-           mod, bias, x, ust, us, kvs, qs, obuf, osnd, ut, utr, qt, kt, vt, pb, bm, ob, uu, hb,
+def kernel(cfg, lag_bias, z_mine, w_in, w_out, own_tab, prev_tab, sqkv_h, so_h, tqkv_h, to_h, up_h, down_h, late, early,
+           mod, bias, z, zq, nz, wi, wo, x, ust, us, kvs, qs, obuf, osnd, ut, utr, qt, kt, vt, pb, bm, ob, uu, hb,
            sqkv, so, tqkv, to, up, down,
-           us_s, us_r, o_s, o_r, ut_s, ut_r, w_sem, t_sem, credit):
+           us_s, us_r, o_s, o_r, ut_s, ut_r, w_sem, t_sem, z_s, z_r, credit):
     L, S, NC, CH, TK, D, FF, HD, MT, MF, WIN = cfg
     R, HS, RH, G = CH * TK, CH // 2, CH * TK // 2, TK // SUB
     CR = CH * SUB
@@ -57,6 +62,7 @@
     DT = D // W
     FT = min(256, FF)
     qscale = HD ** -0.5
+    NCH = w_in.shape[0]
     SU, TU, RS = min(2, HS), min(8, G), min(64, 4 * TK)
 
     vid = lax.axis_index("videos")
@@ -89,6 +95,18 @@
     for layer in range(L):
         t_copy(layer).start()
 
+    wi[...] = jnp.zeros_like(wi)
+    wo[...] = jnp.zeros_like(wo)
+    wi[0:NCH] = w_in[...]
+    wo[0:NCH] = w_out[...]
+    for ref in (z, nz):
+        ref[...] = jnp.zeros_like(ref)
+    for k in range(NC * CH):
+        i, lanes = k // CH, slice(k % CH * TK, (k % CH + 1) * TK)
+        z[i, 0:NCH, lanes] = z_mine[k]
+    for k in range(S):
+        for a in range(CH):
+            nz[k, 0:NCH, a * TK:(a + 1) * TK] = z_mine[NC * CH + k]
     barrier = pltpu.get_barrier_semaphore()
     for dev in (sib, par_a, par_b, nxt, prv):
         pl.semaphore_signal(barrier, inc=1, device_id=dev, device_id_type=MESH)
@@ -113,11 +131,15 @@
         def part(row):
             act(remote(ut.at[i, row:R], utr.at[par, i, row:R], ut_s.at[i], ut_r.at[par, i], nxt))
 
-        pl.when(i == 0)(lambda: part(unread))
-        pl.when(i > 0)(lambda: part(0))
-
-    z[...] = z_in[...]
-    emit[...] = jnp.zeros_like(emit)
+        if isinstance(i, int):
+            part(unread if i == 0 else 0)
+        else:
+            pl.when(i == 0)(lambda: part(unread))
+            pl.when(i > 0)(lambda: part(0))
+
+    near = [remote(z, zq.at[k], z_s.at[k], z_r.at[k], dev) for k, dev in enumerate((sib, par_a, par_b))]
+    for c in near:
+        c.start()
     if unread:
         utr[:, 0, 0:unread, :] = jnp.zeros((2, unread, D), BF)
     for g in range(G):
@@ -138,6 +160,8 @@
             bias[lh // HP, lh % HP, hd * CR:(hd + 1) * CR, :] = tile
 
     for c in tables:
+        c.wait()
+    for c in near:
         c.wait()
 
     lane = lax.broadcasted_iota(jnp.int32, (1, LANES), 1)
@@ -237,7 +261,7 @@
                     ref = kt if kind == 1 else vt
                     ref[g, pl.ds(pl.multiple_of(SR + i * CR, CR), CR), tt * W:(tt + 1) * W] = yg
 
-    def temporal(i, par, layer, step):
+    def halo_kv(i, par, layer):
         ut_each(par, i, lambda c: c.wait())
         uv = utr[par, i]
         for t in range(2 * DT):
@@ -247,6 +271,8 @@
             y4 = y.reshape(CH, G, SUB, W)
             for g in range(G):
                 ref[g, pl.ds(pl.multiple_of(i * CR, CR), CR), tt * W:(tt + 1) * W] = y4[:, g].reshape(CR, W).astype(BF)
+
+    def temporal(i, layer, step):
         rows = lax.broadcasted_iota(jnp.int32, (2 * CR, WIN), 0)
         keys = lax.broadcasted_iota(jnp.int32, (2 * CR, WIN), 1)
         pos_q = i * CH + (rows & (CR - 1)) // SUB
@@ -282,57 +308,58 @@
                     rows = slice(a * TK + g0 * SUB, a * TK + (g0 + gn) * SUB)
                     x[i, rows, cols] = x[i, rows, cols] + y4[:, a].reshape(gn * SUB, W)
 
-    def mlp(i, layer, step):
-        for a in range(CH):
+    def mlp(i, layer, step, r0, r1):
+        for a in range(r0 // TK, r1 // TK):
             def put(r, v, a=a):
                 uu[a * TK + r:a * TK + r + NR, :] = v
 
             modulated(i, a, layer, step, 2, put)
-        uv = uu[...]
         for t in range(FF // FT):
-            hp = mm(uv, up[:, t * FT:(t + 1) * FT])
-            for r in range(0, R, min(R, 128)):
-                hb[r:r + 128, t * FT:(t + 1) * FT] = gelu(hp[r:r + 128]).astype(BF)
-        for r in range(0, R, R // 2):
+            for r in range(r0, r1, RH):
+                hb[r:r + RH, t * FT:(t + 1) * FT] = gelu(mm(uu[r:r + RH], up[:, t * FT:(t + 1) * FT])).astype(BF)
+        for r in range(r0, r1, RH):
             for t in range(DT):
                 cols = slice(t * W, (t + 1) * W)
-                x[i, r:r + R // 2, cols] = x[i, r:r + R // 2, cols] + mm(hb[r:r + R // 2], down[:, cols])
+                x[i, r:r + RH, cols] = x[i, r:r + RH, cols] + mm(hb[r:r + RH], down[:, cols])
 
     def embed(zv):
-        return mm(zv.astype(BF), w_in[...]).astype(BF).astype(F32)
-
-    def ready(i, layer, step):
-        for a in range(CH):
+        return tt_mm(zv.astype(BF), wi[...]).astype(BF).astype(F32)
+
+    def ready(i, layer, step, r0=0, r1=R):
+        for a in range(r0 // TK, r1 // TK):
             def put(r, v, a=a):
                 ust[i, a // HS, (a % HS) * TK + r:(a % HS) * TK + r + NR, :] = v
 
             modulated(i, a, layer, step, 0, put)
 
+    place = lax.broadcasted_iota(jnp.int32, (1, R), 1) // TK
+
     def turn(i, step):
-        for r in range(0, R, RH):
-            for q in range(r, r + RH, NR):
-                uu[q:q + NR, :] = norm(x[i, q:q + NR, :]).astype(BF)
-            v = mm(uu[r:r + RH], w_out[...])
-            entering = []
-            for a in range(r // TK, (r + RH) // TK):
-                dt = mod[i * CH + a + (S - 1) - step, pl.ds(6 * L, 1), 0:LANES]
-                zv = z[i, a * TK:(a + 1) * TK, :] + dt * v[a * TK - r:(a + 1) * TK - r]
-                z[i, a * TK:(a + 1) * TK, :] = zv
-                entering.append(jnp.where(first & (i * CH + a == step), noise[step], zv))
-            x[i, r:r + RH, :] = embed(jnp.concatenate(entering, axis=0))
+        for q in range(0, R, NR):
+            uu[q:q + NR, :] = norm(x[i, q:q + NR, :]).astype(BF)
+        dt = jnp.zeros((1, R), F32)
+        for a in range(CH):
+            dt = jnp.where(place == a, mod[i * CH + a + (S - 1) - step, pl.ds(6 * L, 1), 0:R], dt)
+        zv = z[i] + dt * mm_t(wo[...], uu[...])
+        z[i] = zv
+        x[i] = embed(jnp.where(first & (i * CH + place == step), nz[step], zv))
 
     def replace_head(step):
-        rows = pl.ds(pl.multiple_of((step % CH) * TK, TK), TK)
-        zv = z[step // CH, rows, :]
-        emit[step] = zv
-        z[step // CH, rows, :] = jnp.where(first, noise[step], zv)
+        i = step // CH
+        zv = z[i]
+        for a in range(CH):
+            @pl.when(step % CH == a)
+            def _(a=a):
+                late[NC * CH - S + step] = zv[0:NCH, a * TK:(a + 1) * TK]
+
+        z[i] = jnp.where(first & (i * CH + place == step), nz[step], zv)
 
     def begin(i):
         x[i] = embed(z[i])
         ready(i, 0, 0)
         mine = pl.ds(pl.multiple_of(core * RH, RH), RH)
         for k in range(3):
-            xv = embed(z_near[k, i, mine, :])
+            xv = embed(zq[k, i, :, mine])
             for s in range(HS):
                 gain, shift = affine(i * CH + core * HS + s, 0, 0, 0)
                 us[0, i, k, s * TK:(s + 1) * TK, :] = (norm(xv[s * TK:(s + 1) * TK]) * gain + shift).astype(BF)
@@ -358,6 +385,10 @@
 
             @pl.loop(0, NC + 1)
             def _(c):
+                @pl.when(c == NC - 1)
+                def _():
+                    halo_kv(NC - 1, par, layer)
+
                 @pl.when(c < NC)
                 def _():
                     spatial(NC - 1 - c, par, n)
@@ -378,29 +409,59 @@
                 w_copy(0, nlayer).start()
                 w_copy(1, nlayer).start()
 
-        @pl.loop(0, NC)
-        def _(c):
-            i = NC - 1 - c
-
-            @pl.when(m == 0)
+        @pl.when(m == 0)
+        def _():
+            @pl.loop(0, NC)
+            def _(c):
+                begin(NC - 1 - c)
+
+        def finish_step(i):
+            turn(i, step)
+            ready(i, nlayer, jnp.minimum(nstep, S - 1))
+
+            @pl.when(m < NT)
             def _():
-                begin(i)
-
-            @pl.when(m > 0)
+                for c in us_copies(npar, i):
+                    c.start()
+
+        @pl.when(m > 0)
+        def _():
+            i = NC - 1
+            temporal(i, layer, step)
+            for h in range(2):
+                mlp(i, layer, step, h * RH, (h + 1) * RH)
+                ready(i, nlayer, jnp.minimum(nstep, S - 1), h * RH, (h + 1) * RH)
+                to_sib, to_a, to_b = us_copies(npar, i)
+
+                @pl.when((layer < L - 1) & (core == h))
+                def _():
+                    to_a.start()
+
+                @pl.when((layer < L - 1) & (core != h))
+                def _():
+                    to_b.start()
+                    to_sib.start()
+
+            @pl.when(layer == L - 1)
             def _():
-                temporal(i, par, layer, step)
-                mlp(i, layer, step)
+                finish_step(i)
+
+            @pl.loop(1, NC)
+            def _(c):
+                i = NC - 1 - c
+                halo_kv(i, par, layer)
+                temporal(i, layer, step)
+                mlp(i, layer, step, 0, R)
                 ready(i, nlayer, jnp.minimum(nstep, S - 1))
 
+                @pl.when(layer < L - 1)
+                def _():
+                    for copy in us_copies(npar, i):
+                        copy.start()
+
                 @pl.when(layer == L - 1)
                 def _():
-                    turn(i, step)
-                    ready(i, nlayer, jnp.minimum(nstep, S - 1))
-
-                @pl.when(m < NT)
-                def _():
-                    for c in us_copies(npar, i):
-                        c.start()
+                    finish_step(i)
 
         @pl.when((m > 0) & (layer == L - 1))
         def _():
@@ -411,6 +472,12 @@
             pl.semaphore_signal(credit, inc=1, device_id=prv, device_id_type=MESH)
 
     pl.semaphore_wait(credit, min(2, NT))
+    for k in range(NC * CH):
+        zv = z[k // CH, 0:NCH, k % CH * TK:(k % CH + 1) * TK]
+        if k < S:
+            early[k] = zv
+        else:
+            late[k - S] = zv
 
 
 def denoise_call(cfg, vmem, *args):
@@ -418,10 +485,16 @@
     R, HS, RH, G = CH * TK, CH // 2, CH * TK // 2, TK // SUB
     CR, SR = CH * SUB, NC * CH * SUB
     HP = D // LANES
+    C = args[2].shape[0]
     KR = (NC - 1) * CR + WIN
     scr = [
         pltpu.VMEM((S - 1 + NC * CH, 6 * L + 1, D), F32),
         pltpu.VMEM((L, HP, 2 * CR, WIN), F32),
+        pltpu.VMEM((NC, CPAD, R), F32),
+        pltpu.VMEM((3, NC, CPAD, R), F32),
+        pltpu.VMEM((S, CPAD, R), F32),
+        pltpu.VMEM((CPAD, D), BF),
+        pltpu.VMEM((CPAD, D), BF),
         pltpu.VMEM((NC, R, D), F32),
         pltpu.VMEM((NC, 2, RH, D), BF),
         pltpu.VMEM((2, NC, 3, RH, D), BF),
@@ -453,14 +526,16 @@
         pltpu.SemaphoreType.DMA((2, NC)),
         pltpu.SemaphoreType.DMA((5 + L,)),
         pltpu.SemaphoreType.DMA((2,)),
+        pltpu.SemaphoreType.DMA((3,)),
+        pltpu.SemaphoreType.DMA((3,)),
         pltpu.SemaphoreType.REGULAR,
     ]
     inner = pl.BlockSpec(memory_space=pltpu.VMEM)
     outer = pl.BlockSpec(memory_space=pl.ANY)
     return pl.pallas_call(
         functools.partial(kernel, cfg),
-        out_shape=(jax.ShapeDtypeStruct((NC, R, LANES), F32), jax.ShapeDtypeStruct((S, TK, LANES), F32)),
-        in_specs=[pl.BlockSpec(memory_space=pltpu.SMEM)] + [inner] * 5 + [outer] * 8,
+        out_shape=(jax.ShapeDtypeStruct((NC * CH, C, TK), F32), jax.ShapeDtypeStruct((S, C, TK), F32)),
+        in_specs=[pl.BlockSpec(memory_space=pltpu.SMEM)] + [inner] * 3 + [outer] * 8,
         out_specs=(inner, inner),
         scratch_shapes=scr,
         compiler_params=pltpu.CompilerParams(collective_id=0, has_side_effects=True, vmem_limit_bytes=vmem),
@@ -484,7 +559,6 @@
 
     places = [(blk, q) for blk in range(MF) for q in range(MT)]
     to_seat = [(q * MF + blk, seat(blk, q)) for blk, q in places]
-    to_near = [[((q ^ k) * MF + blk, seat(blk, q)) for blk, q in places] for k in (1, 2, 3)]
     to_home = [(seat(blk, q), q * MF + blk) for blk, q in places]
     to_home_before = [(seat(blk, q), q * MF + (blk - 1) % MF) for blk, q in places]
 
@@ -498,11 +572,8 @@
         WIN = 2 * SL * SUB
         tok, frm, chip, core, odd, half = roles(MT, MF)
         both = ("tokens", "frames")
-        zn = jnp.concatenate([z_loc.reshape(SL, TK * C), noise_loc.reshape(S, TK * C)], axis=0)
-        zn = lax.ppermute(zn, both, to_seat)
-        z_all = jnp.concatenate([zn[:SL]] + [lax.ppermute(z_loc.reshape(SL, TK * C), both, p) for p in to_near], axis=0).reshape(4, SL, TK, C)
-        noise = zn[SL:].reshape(S, TK, C)
-        pad = lambda v: jnp.pad(v, ((0, 0),) * (v.ndim - 1) + ((0, LANES - C),))
+        z_t, noise_t = jnp.swapaxes(z_loc, 1, 2), jnp.swapaxes(noise_loc, 1, 2)
+        z_mine = lax.ppermute(jnp.concatenate([z_t, noise_t], axis=0), both, to_seat)
 
         table = jnp.concatenate([jnp.swapaxes(mod_loc, 1, 2).reshape(SL, 6 * L, D), jnp.broadcast_to(step_loc[:, None, None], (SL, 1, D))], axis=1)
         table_sib = lax.ppermute(table, "frames", to_sib)
@@ -513,22 +584,18 @@
         prev_tab = jnp.where(odd == 0, tail, even_blk[SL - (S - 1):])
 
         by_output = lambda w: jnp.transpose(w, (0, 2, 3, 4, 1)).reshape(L, 3 * D, D)
-        z_tiles = pad(z_all).reshape(4, NC, CH * TK, LANES)
         cfg = (L, S, NC, CH, TK, D, FF, HD, MT, MF, WIN)
-        z_new, emit = denoise_call(
+        late, early = denoise_call(
             cfg, 67043328,
-            lag_bias.reshape(L * lag_bias.shape[1], -1), z_tiles[0], z_tiles[1:], pad(noise),
-            jnp.pad(w_in, ((0, LANES - C), (0, 0))), jnp.pad(w_out, ((0, 0), (0, LANES - C))), own_tab, prev_tab,
+            lag_bias.reshape(L * lag_bias.shape[1], -1), z_mine, w_in, jnp.transpose(w_out), own_tab, prev_tab,
             by_output(w_sqkv), w_so.reshape(L, D, D), by_output(w_tqkv), w_to.reshape(L, D, D), w_up, w_down,
         )
 
-        mine = jnp.concatenate([z_new.reshape(SL, TK, LANES)[:, :, :C].reshape(SL, TK * C), emit[:, :, :C].reshape(S, TK * C)], axis=0)
-        late = lax.ppermute(mine[S:], both, to_home)
-        early = lax.ppermute(mine[:S], both, to_home_before)
-        z_fin = jnp.concatenate([late[:SL - S], early], axis=0).reshape(SL, TK, C)
-        per = TK // MF
-        em = jnp.swapaxes(late[SL - S:].reshape(S, MF, per * C), 0, 1)
-        em = lax.all_to_all(em, "frames", 0, 0, tiled=True)[0].reshape(S, per, C)
+        late = lax.ppermute(late, both, to_home)
+        early = lax.ppermute(early, both, to_home_before)
+        z_fin = jnp.swapaxes(jnp.concatenate([late[:SL - S], early], axis=0), 1, 2)
+        em = jnp.moveaxis(late[SL - S:].reshape(S, C, MF, TK // MF), 2, 0)
+        em = jnp.swapaxes(lax.all_to_all(em, "frames", 0, 0, tiled=True)[0], 1, 2)
         return em, z_fin
 
     return jax.shard_map(body, mesh=mesh, in_specs=(slot_spec, mod_spec, step_spec, noise_spec) + (P(),) * 9, out_specs=(emit_spec, slot_spec), check_vma=False)

time: 675 us -> 655 us (0.970)
  local copies, waits for them, and re-layouts: 45.6 us -> 5.39 us
  Pallas kernels: 594 us -> 620 us
  starting transfers between devices: 26.9 us -> 17.8 us
    slice x10 -> x2, local copies, waits for them, and re-layouts: 31.3 us -> 0.01 us  [the longest x1 0.01 us: body(): z_fin = jnp.swapaxes(jnp.concatenate([late[:SL - S], early], axis=0), 1, 2)]
    pallas_call x1, Pallas kernels: 594 us -> 620 us  [denoise_call(): pl.pallas_call(functools.partial(kernel, cfg), out_shape=(jax.ShapeDtypeS...]
    ppermute x6 -> x3, starting transfers between devices: 22.4 us -> 11.5 us  [the longest x1 6.84 us: body(): lax.ppermute(jnp.concatenate([z_t, noise_t], axis=0), both, to_seat)]
  transfers between devices with their start and end apart: 9 -> 6, of which waited for: 1 -> 4; matrix products, arithmetic and copies ran while one was open for 6% -> 0% of each run, Pallas kernels for 0% -> 0%
where the time goes in v4:
time: 655 us; the launch traced here: 654 us
  Pallas kernels  620 us (95%)
  starting transfers between devices  17.8 us (3%)
  waiting for transfers between devices  7.02 us (1%)
    pallas_call x1, Pallas kernels, denoise_call(): pl.pallas_call(functools.partial(kernel, cfg), out_shape=(jax.ShapeDtypeS...  620 us
  transfers between devices with their start and end apart: 6, of which 4 were waited for; matrix products, arithmetic and copies ran while one was open for 0% of the time, Pallas kernels for 0%

profile of v4, /device:TPU:97, one launch (start us, length us, event | category | flops | bytes accessed | tf_op | source)
XLA Modules:
  0.0 654.4 jit_solution(1342221883848955605)
XLA Ops:
  0.6 0.0 copy-start
  0.6 0.0 copy-start.2
  0.7 0.0 copy-start.1
  0.7 1.2 copy.23
  1.9 0.4 copy.24
  2.2 0.7 broadcast_in_dim.2
  3.0 0.1 pad_maximum_fusion
  3.1 0.4 copy.25
  3.5 2.1 collective-permute-start.1
  5.6 1.7 collective-permute-done.1
  7.3 1.4 broadcast_select_fusion
  8.7 0.8 collective-permute-start.2
  9.5 0.0 copy-done
  9.5 0.0 copy-done.2
  9.5 6.8 %collective-permute-start = (f32[22,4,64]{2,1,0:T(4,128)S(1)}, f32[22,4,64]{2,1,0:T(4,128)}, u32[]{:S(2)}, u32[]{:S(2)}) collective-permute-start(f32[22,4,64]{2,1,0:T(4,128)S(1)} %pad_maximum_fusion.1), channel_id=1, source_target_pairs={{0,0},{8,1},{16,8},{24,9},{1,24},{9,25},{17,16},{25,17},{2,26},{10... | collective-permute-start | bytes 67592 | tf_op jit(solution)/shard_map/ppermute | solution.py:576
  16.4 0.0 copy-done.1
  16.4 0.6 reshape.35.lag_bias
  17.0 0.1 collective-permute-done.2
  17.1 0.7 slice_select_fusion.prev_tab
  17.8 0.0 collective-permute-done.z_mine
  17.8 619.8 %fifo_denoise.1 = (f32[16,4,64]{2,1,0:T(4,128)}, f32[6,4,64]{2,1,0:T(4,128)}) custom-call(f32[24,16]{1,0:T(8,128)} %reshape.35.lag_bias, f32[22,4,64]{2,1,0:T(4,128)} %collective-permute-done.z_mine, bf16[4,768]{1,0:T(4,128)(2,1)} %w_in.1, bf16[4,768]{1,0:T(4,128)(2,1)} %bitcast.31, f32[16,13,768]{2,1,0:T(8,128)} %get-tuple-element.6.own_tab, ...), custom_call_target="tpu_custom_call" | custom-call | tf_op jit(solution)/shard_map/fifo_denoise/pallas_call | solution.py:535
  637.7 2.0 collective-permute-start.3
  639.6 2.7 collective-permute-start.4
  642.3 1.8 collective-permute-done.3
  644.1 0.1 reshape.34
  644.3 0.7 reshape.36
  645.0 3.4 all-to-all-start
  648.4 0.0 collective-permute-done.4
  648.5 0.6 maximum_bitcast_fusion
  649.1 3.4 all-to-all-done
  652.5 0.5 broadcast.6
  653.0 0.7 reduce
  653.6 0.1 reshape.37
  653.8 0.6 slice_bitcast_fusion
  (6 shorter events, 0.1 us)
Async XLA Ops:
  0.6 8.9 %copy-start = (f32[16,64,4]{1,2,0:T(4,128)S(1)}, f32[16,64,4]{1,2,0:T(4,128)}, u32[]{:S(2)}) copy-start(f32[16,64,4]{1,2,0:T(4,128)} %param.13) | copy-start | bytes 49156
  0.6 8.9 %copy-start.2 = (f32[6,64,4]{1,2,0:T(4,128)S(1)}, f32[6,64,4]{1,2,0:T(4,128)}, u32[]{:S(2)}) copy-start(f32[6,64,4]{1,2,0:T(4,128)} %param.16) | copy-start | bytes 18436
  0.7 15.7 %copy-start.1 = (f32[2,12,16]{2,0,1:T(2,128)S(1)}, f32[2,12,16]{2,0,1:T(2,128)}, u32[]{:S(2)}) copy-start(f32[2,12,16]{2,0,1:T(2,128)} %param.17) | copy-start | bytes 4612
  3.5 3.8 collective-permute-start.1
  8.7 8.4 %collective-permute-start.2 = (f32[5,13,768]{2,1,0:T(8,128)S(1)}, f32[5,13,768]{2,1,0:T(8,128)S(1)}, u32[]{:S(2)}, u32[]{:S(2)}) collective-permute-start(f32[5,13,768]{2,1,0:T(8,128)S(1)} %slice.20), channel_id=1, source_target_pairs={{0,2},{1,3},{2,4},{3,5},{4,6},{5,7},{6,0},{7,1},{8,10},{9,11},{10,... | collective-permute-start | bytes 599048 | tf_op jit(solution)/shard_map/ppermute | solution.py:582
  9.5 8.3 %collective-permute-start = (f32[22,4,64]{2,1,0:T(4,128)S(1)}, f32[22,4,64]{2,1,0:T(4,128)}, u32[]{:S(2)}, u32[]{:S(2)}) collective-permute-start(f32[22,4,64]{2,1,0:T(4,128)S(1)} %pad_maximum_fusion.1), channel_id=1, source_target_pairs={{0,0},{8,1},{16,8},{24,9},{1,24},{9,25},{17,16},{25,17},{2,26},{10... | collective-permute-start | bytes 67592 | tf_op jit(solution)/shard_map/ppermute | solution.py:576
  637.7 6.5 collective-permute-start.3
  639.6 8.8 %collective-permute-start.4 = (f32[6,4,64]{2,1,0:T(4,128)}, f32[6,4,64]{2,1,0:T(4,128)S(1)}, u32[]{:S(2)}, u32[]{:S(2)}) collective-permute-start(f32[6,4,64]{2,1,0:T(4,128)} %get-tuple-element.5), channel_id=1, source_target_pairs={{0,7},{1,15},{8,23},{9,31},{24,0},{25,8},{16,16},{17,24},{26,1},{2... | collective-permute-start | bytes 18440 | tf_op jit(solution)/shard_map/ppermute | solution.py:595
  645.0 7.4 %all-to-all-start = ((f32[8,1,192]{2,1,0:T(1,128)}), f32[8,1,192]{2,1,0:T(1,128)S(1)}, u32[]{:S(2)}, u32[]{:S(2)}) async-start(f32[8,1,192]{2,1,0:T(1,128)} %reshape.36), calls=%async_computation | async-start | bytes 16384 | tf_op jit(solution)/shard_map/all_to_all | solution.py:598

commit v5 on v4

--- a/solution.py
+++ b/solution.py
@@ -131,11 +131,8 @@
         def part(row):
             act(remote(ut.at[i, row:R], utr.at[par, i, row:R], ut_s.at[i], ut_r.at[par, i], nxt))
 
-        if isinstance(i, int):
-            part(unread if i == 0 else 0)
-        else:
-            pl.when(i == 0)(lambda: part(unread))
-            pl.when(i > 0)(lambda: part(0))
+        pl.when(i == 0)(lambda: part(unread))
+        pl.when(i > 0)(lambda: part(0))
 
     near = [remote(z, zq.at[k], z_s.at[k], z_r.at[k], dev) for k, dev in enumerate((sib, par_a, par_b))]
     for c in near:
@@ -261,7 +258,7 @@
                     ref = kt if kind == 1 else vt
                     ref[g, pl.ds(pl.multiple_of(SR + i * CR, CR), CR), tt * W:(tt + 1) * W] = yg
 
-    def halo_kv(i, par, layer):
+    def temporal(i, par, layer, step):
         ut_each(par, i, lambda c: c.wait())
         uv = utr[par, i]
         for t in range(2 * DT):
@@ -271,8 +268,6 @@
             y4 = y.reshape(CH, G, SUB, W)
             for g in range(G):
                 ref[g, pl.ds(pl.multiple_of(i * CR, CR), CR), tt * W:(tt + 1) * W] = y4[:, g].reshape(CR, W).astype(BF)
-
-    def temporal(i, layer, step):
         rows = lax.broadcasted_iota(jnp.int32, (2 * CR, WIN), 0)
         keys = lax.broadcasted_iota(jnp.int32, (2 * CR, WIN), 1)
         pos_q = i * CH + (rows & (CR - 1)) // SUB
@@ -308,25 +303,25 @@
                     rows = slice(a * TK + g0 * SUB, a * TK + (g0 + gn) * SUB)
                     x[i, rows, cols] = x[i, rows, cols] + y4[:, a].reshape(gn * SUB, W)
 
-    def mlp(i, layer, step, r0, r1):
-        for a in range(r0 // TK, r1 // TK):
+    def mlp(i, layer, step):
+        for a in range(CH):
             def put(r, v, a=a):
                 uu[a * TK + r:a * TK + r + NR, :] = v
 
             modulated(i, a, layer, step, 2, put)
         for t in range(FF // FT):
-            for r in range(r0, r1, RH):
+            for r in range(0, R, RH):
                 hb[r:r + RH, t * FT:(t + 1) * FT] = gelu(mm(uu[r:r + RH], up[:, t * FT:(t + 1) * FT])).astype(BF)
-        for r in range(r0, r1, RH):
+        for r in range(0, R, R // 2):
             for t in range(DT):
                 cols = slice(t * W, (t + 1) * W)
-                x[i, r:r + RH, cols] = x[i, r:r + RH, cols] + mm(hb[r:r + RH], down[:, cols])
+                x[i, r:r + R // 2, cols] = x[i, r:r + R // 2, cols] + mm(hb[r:r + R // 2], down[:, cols])
 
     def embed(zv):
         return tt_mm(zv.astype(BF), wi[...]).astype(BF).astype(F32)
 
-    def ready(i, layer, step, r0=0, r1=R):
-        for a in range(r0 // TK, r1 // TK):
+    def ready(i, layer, step):
+        for a in range(CH):
             def put(r, v, a=a):
                 ust[i, a // HS, (a % HS) * TK + r:(a % HS) * TK + r + NR, :] = v
 
@@ -385,10 +380,6 @@
 
             @pl.loop(0, NC + 1)
             def _(c):
-                @pl.when(c == NC - 1)
-                def _():
-                    halo_kv(NC - 1, par, layer)
-
                 @pl.when(c < NC)
                 def _():
                     spatial(NC - 1 - c, par, n)
@@ -409,59 +400,29 @@
                 w_copy(0, nlayer).start()
                 w_copy(1, nlayer).start()
 
-        @pl.when(m == 0)
-        def _():
-            @pl.loop(0, NC)
-            def _(c):
-                begin(NC - 1 - c)
-
-        def finish_step(i):
-            turn(i, step)
-            ready(i, nlayer, jnp.minimum(nstep, S - 1))
-
-            @pl.when(m < NT)
+        @pl.loop(0, NC)
+        def _(c):
+            i = NC - 1 - c
+
+            @pl.when(m == 0)
             def _():
-                for c in us_copies(npar, i):
-                    c.start()
-
-        @pl.when(m > 0)
-        def _():
-            i = NC - 1
-            temporal(i, layer, step)
-            for h in range(2):
-                mlp(i, layer, step, h * RH, (h + 1) * RH)
-                ready(i, nlayer, jnp.minimum(nstep, S - 1), h * RH, (h + 1) * RH)
-                to_sib, to_a, to_b = us_copies(npar, i)
-
-                @pl.when((layer < L - 1) & (core == h))
-                def _():
-                    to_a.start()
-
-                @pl.when((layer < L - 1) & (core != h))
-                def _():
-                    to_b.start()
-                    to_sib.start()
-
-            @pl.when(layer == L - 1)
+                begin(i)
+
+            @pl.when(m > 0)
             def _():
-                finish_step(i)
-
-            @pl.loop(1, NC)
-            def _(c):
-                i = NC - 1 - c
-                halo_kv(i, par, layer)
-                temporal(i, layer, step)
-                mlp(i, layer, step, 0, R)
+                temporal(i, par, layer, step)
+                mlp(i, layer, step)
                 ready(i, nlayer, jnp.minimum(nstep, S - 1))
-
-                @pl.when(layer < L - 1)
-                def _():
-                    for copy in us_copies(npar, i):
-                        copy.start()
 
                 @pl.when(layer == L - 1)
                 def _():
-                    finish_step(i)
+                    turn(i, step)
+                    ready(i, nlayer, jnp.minimum(nstep, S - 1))
+
+                @pl.when(m < NT)
+                def _():
+                    for c in us_copies(npar, i):
+                        c.start()
 
         @pl.when((m > 0) & (layer == L - 1))
         def _():

time: 655 us -> 631 us (0.963)
  Pallas kernels: 620 us -> 596 us
    pallas_call x1, Pallas kernels: 620 us -> 596 us  [denoise_call(): pl.pallas_call(functools.partial(kernel, cfg), out_shape=(jax.ShapeDtypeS...]
where the time goes in v5:
time: 631 us
  Pallas kernels  596 us (94%)
  starting transfers between devices  19.7 us (3%)
    pallas_call x1, Pallas kernels, denoise_call(): pl.pallas_call(functools.partial(kernel, cfg), out_shape=(jax.ShapeDtypeS...  596 us
  transfers between devices with their start and end apart: 6, of which 4 were waited for; matrix products, arithmetic and copies ran while one was open for 0% of the time, Pallas kernels for 0%

profile of v5, /device:TPU:97, one launch (start us, length us, event | category | flops | bytes accessed | tf_op | source)
XLA Modules:
  0.0 631.0 jit_solution(3280271875430359646)
XLA Ops:
  0.6 0.0 copy-start
  0.6 0.0 copy-start.2
  0.7 0.0 copy-start.1
  0.7 1.2 copy.23
  1.9 0.4 copy.24
  2.2 0.7 broadcast_in_dim.2
  3.0 0.1 pad_maximum_fusion
  3.1 0.4 copy.25
  3.5 2.1 collective-permute-start.1
  5.6 1.7 collective-permute-done.1
  7.3 1.4 broadcast_select_fusion
  8.7 0.8 collective-permute-start.2
  9.5 0.0 copy-done
  9.5 0.0 copy-done.2
  9.5 6.8 %collective-permute-start = (f32[22,4,64]{2,1,0:T(4,128)S(1)}, f32[22,4,64]{2,1,0:T(4,128)}, u32[]{:S(2)}, u32[]{:S(2)}) collective-permute-start(f32[22,4,64]{2,1,0:T(4,128)S(1)} %pad_maximum_fusion.1), channel_id=1, source_target_pairs={{0,0},{8,1},{16,8},{24,9},{1,24},{9,25},{17,16},{25,17},{2,26},{10... | collective-permute-start | bytes 67592 | tf_op jit(solution)/shard_map/ppermute | solution.py:537
  16.4 0.0 copy-done.1
  16.4 0.6 reshape.35.lag_bias
  17.0 0.1 collective-permute-done.2
  17.1 0.7 slice_select_fusion.prev_tab
  17.8 0.0 collective-permute-done.z_mine
  17.8 596.0 %fifo_denoise.1 = (f32[16,4,64]{2,1,0:T(4,128)}, f32[6,4,64]{2,1,0:T(4,128)}) custom-call(f32[24,16]{1,0:T(8,128)} %reshape.35.lag_bias, f32[22,4,64]{2,1,0:T(4,128)} %collective-permute-done.z_mine, bf16[4,768]{1,0:T(4,128)(2,1)} %w_in.1, bf16[4,768]{1,0:T(4,128)(2,1)} %bitcast.31, f32[16,13,768]{2,1,0:T(8,128)} %get-tuple-element.6.own_tab, ...), custom_call_target="tpu_custom_call" | custom-call | tf_op jit(solution)/shard_map/fifo_denoise/pallas_call | solution.py:496
  613.9 2.2 collective-permute-start.3
  616.0 4.2 collective-permute-start.4
  620.2 0.1 collective-permute-done.3
  620.3 0.1 reshape.34
  620.5 0.7 reshape.36
  621.2 3.5 all-to-all-start
  624.7 0.0 collective-permute-done.4
  624.7 0.6 maximum_bitcast_fusion
  625.3 3.8 all-to-all-done
  629.1 0.5 broadcast.6
  629.6 0.7 reduce
  630.3 0.1 reshape.37
  630.4 0.6 slice_bitcast_fusion
  (6 shorter events, 0.1 us)
Async XLA Ops:
  0.6 8.9 %copy-start = (f32[16,64,4]{1,2,0:T(4,128)S(1)}, f32[16,64,4]{1,2,0:T(4,128)}, u32[]{:S(2)}) copy-start(f32[16,64,4]{1,2,0:T(4,128)} %param.13) | copy-start | bytes 49156
  0.6 8.9 %copy-start.2 = (f32[6,64,4]{1,2,0:T(4,128)S(1)}, f32[6,64,4]{1,2,0:T(4,128)}, u32[]{:S(2)}) copy-start(f32[6,64,4]{1,2,0:T(4,128)} %param.16) | copy-start | bytes 18436
  0.7 15.7 %copy-start.1 = (f32[2,12,16]{2,0,1:T(2,128)S(1)}, f32[2,12,16]{2,0,1:T(2,128)}, u32[]{:S(2)}) copy-start(f32[2,12,16]{2,0,1:T(2,128)} %param.17) | copy-start | bytes 4612
  3.5 3.8 collective-permute-start.1
  8.7 8.4 %collective-permute-start.2 = (f32[5,13,768]{2,1,0:T(8,128)S(1)}, f32[5,13,768]{2,1,0:T(8,128)S(1)}, u32[]{:S(2)}, u32[]{:S(2)}) collective-permute-start(f32[5,13,768]{2,1,0:T(8,128)S(1)} %slice.20), channel_id=1, source_target_pairs={{0,2},{1,3},{2,4},{3,5},{4,6},{5,7},{6,0},{7,1},{8,10},{9,11},{10,... | collective-permute-start | bytes 599048 | tf_op jit(solution)/shard_map/ppermute | solution.py:543
  9.5 8.3 %collective-permute-start = (f32[22,4,64]{2,1,0:T(4,128)S(1)}, f32[22,4,64]{2,1,0:T(4,128)}, u32[]{:S(2)}, u32[]{:S(2)}) collective-permute-start(f32[22,4,64]{2,1,0:T(4,128)S(1)} %pad_maximum_fusion.1), channel_id=1, source_target_pairs={{0,0},{8,1},{16,8},{24,9},{1,24},{9,25},{17,16},{25,17},{2,26},{10... | collective-permute-start | bytes 67592 | tf_op jit(solution)/shard_map/ppermute | solution.py:537
  613.9 6.5 %collective-permute-start.3 = (f32[16,4,64]{2,1,0:T(4,128)}, f32[16,4,64]{2,1,0:T(4,128)S(1)}, u32[]{:S(2)}, u32[]{:S(2)}) collective-permute-start(f32[16,4,64]{2,1,0:T(4,128)} %get-tuple-element.4), channel_id=1, source_target_pairs={{0,0},{1,8},{8,16},{9,24},{24,1},{25,9},{16,17},{17,25},{26,2},{27... | collective-permute-start | bytes 49160 | tf_op jit(solution)/shard_map/ppermute | solution.py:555
  616.0 8.7 %collective-permute-start.4 = (f32[6,4,64]{2,1,0:T(4,128)}, f32[6,4,64]{2,1,0:T(4,128)S(1)}, u32[]{:S(2)}, u32[]{:S(2)}) collective-permute-start(f32[6,4,64]{2,1,0:T(4,128)} %get-tuple-element.5), channel_id=1, source_target_pairs={{0,7},{1,15},{8,23},{9,31},{24,0},{25,8},{16,16},{17,24},{26,1},{2... | collective-permute-start | bytes 18440 | tf_op jit(solution)/shard_map/ppermute | solution.py:556
  621.2 7.9 %all-to-all-start = ((f32[8,1,192]{2,1,0:T(1,128)}), f32[8,1,192]{2,1,0:T(1,128)S(1)}, u32[]{:S(2)}, u32[]{:S(2)}) async-start(f32[8,1,192]{2,1,0:T(1,128)} %reshape.36), calls=%async_computation | async-start | bytes 16384 | tf_op jit(solution)/shard_map/all_to_all | solution.py:559
